TPU v7x, 32 devices: a whole 2x2x4 slice. The times are simulated.
32 devices in a mesh: dp: 8 (over z, x), expert: 4 (over y, core).
Axes of the slice: x: 2, y: 2, z: 4, core: 2. Of those that a mesh axis runs over, the one named last changes fastest.
Arguments:
- queries: bfloat16 [256, 2048], P(('dp', 'expert')), may hold values from -8 to 8
- fresh_key: bfloat16 [256, 256], P(('dp', 'expert')), may hold values from -4 to 4
- fresh_value: bfloat16 [256, 256], P(('dp', 'expert')), may hold values from -4 to 4
- cached_keys: bfloat16 [256, 128, 256], P(('dp', 'expert')), may hold values from -8 to 8
- cached_values: bfloat16 [256, 128, 256], P(('dp', 'expert')), may hold values from -4 to 4
- lengths: int32 [256], P(('dp', 'expert')), may hold values from 2 to 128
- sink_logit_rows: float32 [32], replicated, may hold values from 1 to 5
- residual: bfloat16 [256, 2880], P('dp', 'expert'), may hold values from -6 to 6
- o_weight: bfloat16 [2880, 2048], P('expert'), may hold values from -0.125 to 0.125
- norm_gain: float32 [2880], replicated, may hold values from 0.5 to 1.5
- expert_ids: int32 [256, 4], replicated, may hold values from 0 to 7, all different within a row; in each aligned block of 32 rows (0 to 31, 32 to 63, ...) at most 32 rows name the same one
- route_weights: float32 [256, 4], replicated, may hold values from 0.1 to 0.6
- w_gate_up: bfloat16 [8, 2, 2880, 2880], P('dp', None, 'expert'), may hold values from -0.109375 to 0.109375
- w_down: bfloat16 [8, 2880, 2880], P('dp', 'expert'), may hold values from -0.15625 to 0.15625
Outputs:
- layer_out: bfloat16 [256, 2880], P('dp', 'expert')
Inputs may be any that keep to these rules, and one draw needn't show every extreme that they name: `expert_ids`: each row names 4 different experts; among any aligned block of 32 rows no expert is named by more than 32 rows.
All inputs are finite; a program needn't handle non-finite values.
Results may differ from a plain program's by a relative error of at most 0.018.
Values may be sent and summed in bfloat16 or wider, within the bound.
No kernel may reach another device: no remote copies, remote signals or barrier semaphores. Data moves between devices by JAX's collectives and lax.ppermute only.
A program may use at most 64 MiB of HBM per device.

v0:
```python
import functools
import math

import jax
import jax.numpy as jnp
from jax import lax
from jax.experimental import pallas as pl
from jax.experimental.pallas import tpu as pltpu
from jax.sharding import PartitionSpec as P


D = 2880
QUERY_HEADS = 32
KEY_VALUE_HEADS = 4
HEAD_SIZE = 64
WINDOW_LENGTH = 128
TOP = 4


norm_eps = 1e-05
swish_alpha = 1.702
MIB = 1 << 20


def attend_kernel(
    len_hbm, sink_hbm, q_hbm, fk_hbm, fv_hbm, ck_hbm, cv_hbm, gu_hbm,
    out_ref, gu_ref, len_ref, sink_ref, q_ref, fk_ref, fv_ref, ck_ref, cv_ref, qs_ref, os_ref, sem
):
    ins = [
        (q_hbm, q_ref), (len_hbm, len_ref), (sink_hbm, sink_ref), (fk_hbm, fk_ref), (fv_hbm, fv_ref),
        (ck_hbm, ck_ref), (cv_hbm, cv_ref)
    ]
    ahead = [(gu_hbm.at[:, 0], gu_ref)]
    copies = [pltpu.make_async_copy(src, dst, sem.at[n]) for n, (src, dst) in enumerate(ins + ahead)]
    for copy in copies:
        copy.start()
    batch, width = q_ref.shape
    heads = sink_ref.shape[0]
    size = width // heads
    kv_heads = fk_ref.shape[1] // size
    group = heads // kv_heads
    window = ck_ref.shape[1]
    scale = 1.0 / math.sqrt(size)
    qs_ref[...] = jnp.zeros(qs_ref.shape, jnp.float32)
    slots = lax.broadcasted_iota(jnp.int32, (heads, window), 1)
    head_rows = lax.broadcasted_iota(jnp.int32, (heads, 1), 0)
    copies[0].wait()
    q = q_ref[...].astype(jnp.float32)
    for h in range(heads):
        k = h // group
        qs_ref[:, h, k * size:(k + 1) * size] = q[:, h * size:(h + 1) * size]
    for copy in copies[1:5]:
        copy.wait()
    sink = jnp.zeros((heads, 1), jnp.float32)
    for h in range(heads):
        sink = jnp.where(head_rows == h, sink_ref[h], sink)
    fk = fk_ref[...].astype(jnp.float32)
    fv = fv_ref[...].astype(jnp.float32)
    copies[5].wait()
    scores, owns = [], []
    for b in range(batch):
        qb = qs_ref[b]
        score = lax.dot_general(
            qb.astype(jnp.bfloat16), ck_ref[b], (((1,), (1,)), ((), ())), preferred_element_type=jnp.float32
        ) * scale
        scores.append(jnp.where(slots >= window - len_ref[b], score, -jnp.inf))
        owns.append(jnp.sum(qb * fk[b:b + 1], axis=1, keepdims=True) * scale)
    scores = jnp.concatenate(scores, axis=0)
    own = jnp.concatenate(owns, axis=0)
    sink = jnp.concatenate([sink] * batch, axis=0)
    top = jnp.maximum(jnp.maximum(jnp.max(scores, axis=1, keepdims=True), own), sink)
    probs = jnp.exp(scores - top)
    own = jnp.exp(own - top)
    total = jnp.sum(probs, axis=1, keepdims=True) + own + jnp.exp(sink - top)
    share = 1.0 / total
    probs = (probs * share).astype(jnp.bfloat16)
    own = (own * share).astype(jnp.bfloat16).astype(jnp.float32)
    copies[6].wait()
    for b in range(batch):
        part = slice(b * heads, (b + 1) * heads)
        os_ref[b] = jnp.dot(probs[part], cv_ref[b], preferred_element_type=jnp.float32) + own[part] * fv[b:b + 1]
    for h in range(0, heads, 2):
        k0 = h // group
        k1 = (h + 1) // group
        pair = jnp.concatenate(
            [os_ref[:, h, k0 * size:(k0 + 1) * size], os_ref[:, h + 1, k1 * size:(k1 + 1) * size]], axis=1
        )
        out_ref[:, h * size:(h + 2) * size] = pair.astype(jnp.bfloat16)
    for copy in copies[len(ins):]:
        copy.wait()


VMEM = pl.BlockSpec(memory_space=pltpu.VMEM)
SMEM = pl.BlockSpec(memory_space=pltpu.SMEM)
HBM = pl.BlockSpec(memory_space=pltpu.HBM)


def in_hbm(array):
    return pltpu.with_memory_space_constraint(array, pltpu.HBM)


def attend_local(
    queries, fresh_key, fresh_value, cached_keys, cached_values, lengths, sink_logit_rows, w_gate_up
):
    arrays = [queries, fresh_key, fresh_value, cached_keys, cached_values]
    small = [lengths, sink_logit_rows]
    spread = (queries.shape[0], sink_logit_rows.shape[0], fresh_key.shape[1])
    gate_shape = w_gate_up.shape[:1] + w_gate_up.shape[2:]
    return pl.pallas_call(
        attend_kernel,
        out_shape=[jax.ShapeDtypeStruct(shape, jnp.bfloat16) for shape in (queries.shape, gate_shape)],
        in_specs=[HBM] * 8,
        out_specs=[VMEM] * 2,
        scratch_shapes=[pltpu.SMEM(a.shape, a.dtype) for a in small] + [
            pltpu.VMEM(a.shape, a.dtype) for a in arrays
        ] + [
            pltpu.VMEM(spread, jnp.float32),
            pltpu.VMEM(spread, jnp.float32),
            pltpu.SemaphoreType.DMA((8,)),
        ],
        compiler_params=pltpu.CompilerParams(vmem_limit_bytes=32 * MIB),
        name="attend",
    )(*[in_hbm(a) for a in small + arrays + [w_gate_up]])


def bring_kernel(after_ref, source_hbm, target_ref, sem):
    copy = pltpu.make_async_copy(source_hbm, target_ref, sem.at[0])
    copy.start()
    copy.wait()


def bring(after, weight):
    call = pl.pallas_call(
        bring_kernel,
        out_shape=jax.ShapeDtypeStruct(weight.shape, weight.dtype),
        in_specs=[VMEM, HBM],
        out_specs=VMEM,
        scratch_shapes=[pltpu.SemaphoreType.DMA((1,))],
        compiler_params=pltpu.CompilerParams(vmem_limit_bytes=8 * MIB),
        cost_estimate=pl.CostEstimate(flops=10**9, bytes_accessed=4 * MIB, transcendentals=0),
        name="bring",
    )
    weight = in_hbm(weight)
    return call(after, weight)


def project_kernel(*refs):
    blocks, (w_ref, res_ref, out_ref, rows_ref) = refs[:-4], refs[-4:]
    rows = blocks[0].shape[0]
    place = lax.axis_index("expert")
    for r, block in enumerate(blocks):
        rows_ref[pl.ds(pl.multiple_of((place ^ r) * rows, rows), rows), :] = block[...].astype(jnp.float32)
    projected = lax.dot_general(
        rows_ref[...].astype(jnp.bfloat16), w_ref[...], (((1,), (1,)), ((), ())), preferred_element_type=jnp.float32
    )
    out_ref[...] = (res_ref[...].astype(jnp.float32) + projected).astype(jnp.bfloat16)


def project(blocks, o_weight, residual):
    rows, width = blocks[0].shape
    return pl.pallas_call(
        project_kernel,
        out_shape=jax.ShapeDtypeStruct(residual.shape, jnp.bfloat16),
        in_specs=[VMEM] * (len(blocks) + 1) + [pl.BlockSpec(residual.shape, lambda: (0, 0))],
        out_specs=VMEM,
        scratch_shapes=[pltpu.VMEM((rows * len(blocks), width), jnp.float32)],
        compiler_params=pltpu.CompilerParams(vmem_limit_bytes=12 * MIB),
        name="project",
    )(*blocks, o_weight, residual)


def expert_kernel(*refs, lo, ys):
    halves = 2
    pairs = lo * ys
    near, far, (gain_ref, ids_ref, route_ref, gate_ref, gu_hbm, down_hbm) = (
        refs[:pairs], refs[pairs:2 * pairs], refs[2 * pairs:2 * pairs + 6]
    )
    refs = refs[2 * pairs + 6:]
    keep, send = refs[:pairs], refs[pairs:2 * pairs]
    x_ref, weight_ref, up_ref, down_ref, hidden_ref, sums_ref, sem = refs[2 * pairs:]
    span, columns = near[0].shape
    width = x_ref.shape[1]
    members = ys * halves
    group = lax.axis_index("dp")
    place = lax.axis_index("expert")
    up_copy = pltpu.make_async_copy(gu_hbm.at[0, 1], up_ref, sem.at[0])
    down_copy = pltpu.make_async_copy(down_hbm.at[0], down_ref, sem.at[1])
    up_copy.start()
    down_copy.start()

    groups = weight_ref.shape[0]
    tokens = ids_ref.shape[1]
    rows = tokens // groups
    zs = span // rows
    weight = jnp.sum(jnp.where(ids_ref[...] == group, route_ref[...], 0.0), axis=0, keepdims=True)
    weight = jnp.transpose(jnp.broadcast_to(weight, (8, tokens)))[:, :1]
    for g in range(groups):
        weight_ref[g] = weight[g * rows:(g + 1) * rows]

    for p in range(members):
        @pl.when(place == p)
        def _():
            for x in range(lo):
                for r in range(members):
                    j = p ^ r
                    blocks = far if r % halves else near
                    gain = gain_ref[:, j * columns:(j + 1) * columns]
                    v = blocks[x * ys + r // halves][...].astype(jnp.float32)
                    x_ref[x * span:(x + 1) * span, j * columns:(j + 1) * columns] = (v * gain).astype(jnp.bfloat16)

    x_all = x_ref[...]
    contract = (((1,), (1,)), ((), ()))
    gate = lax.dot_general(x_all, gate_ref[0], contract, preferred_element_type=jnp.float32)
    norms = []
    for x in range(lo):
        squares = jnp.zeros((span, columns), jnp.float32)
        for y in range(ys):
            for blocks in (near, far):
                v = blocks[x * ys + y][...].astype(jnp.float32)
                squares = squares + v * v
        norms.append(lax.rsqrt(jnp.sum(squares, axis=1, keepdims=True) / width + norm_eps))
    norm = jnp.concatenate(norms, axis=0)
    gate = gate * norm
    gate = gate * jax.nn.sigmoid(swish_alpha * gate)
    up_copy.wait()
    up = lax.dot_general(x_all, up_ref[...], contract, preferred_element_type=jnp.float32)
    hidden_ref[...] = ((up * norm + 1.0) * gate).astype(jnp.bfloat16)
    down_copy.wait()
    scale = jnp.concatenate([weight_ref[group ^ (z * lo + x)] for x in range(lo) for z in range(zs)], axis=0)
    hidden = hidden_ref[...]
    for i in range(0, width, 768):
        part = slice(i, min(i + 768, width))
        sums_ref[:, part] = (
            jnp.dot(hidden, down_ref[:, part], preferred_element_type=jnp.float32) * scale
        ).astype(jnp.bfloat16)
    for p in range(members):
        @pl.when(place == p)
        def _():
            for x in range(lo):
                for r in range(members):
                    j = p ^ r
                    blocks = send if r % halves else keep
                    blocks[x * ys + r // halves][...] = sums_ref[
                        x * span:(x + 1) * span, j * columns:(j + 1) * columns
                    ]


def expert_sums(near, far, norm_gain, expert_ids, route_weights, w_gate, w_gate_up, w_down, groups, lo):
    units, width = w_down.shape[1:]
    pairs = len(near)
    ys = pairs // lo
    span, columns = near[0].shape
    total = span * lo
    outs = pl.pallas_call(
        functools.partial(expert_kernel, lo=lo, ys=ys),
        out_shape=[jax.ShapeDtypeStruct((span, columns), jnp.bfloat16)] * (2 * pairs),
        in_specs=[VMEM] * (2 * pairs + 4) + [HBM] * 2,
        out_specs=[VMEM] * (2 * pairs),
        scratch_shapes=[
            pltpu.VMEM((total, width), jnp.bfloat16),
            pltpu.VMEM((groups, total // groups, 1), jnp.float32),
            pltpu.VMEM((units, width), jnp.bfloat16),
            pltpu.VMEM((units, width), jnp.bfloat16),
            pltpu.VMEM((total, units), jnp.bfloat16),
            pltpu.VMEM((total, width), jnp.bfloat16),
            pltpu.SemaphoreType.DMA((2,)),
        ],
        compiler_params=pltpu.CompilerParams(vmem_limit_bytes=36 * MIB),
        name="experts",
    )(
        *near, *far, norm_gain[None, :], expert_ids.T, route_weights.T, w_gate, in_hbm(w_gate_up), in_hbm(w_down)
    )
    return outs[:pairs], outs[pairs:]


def dense_body(
    queries, fresh_key, fresh_value, cached_keys, cached_values, lengths, sink_logit_rows, residual, o_weight,
    norm_gain, expert_ids, route_weights, w_gate_up, w_down
):
    groups = lax.axis_size("dp")
    members = lax.axis_size("expert")
    lo, halves = 2, 2
    zs, ys = groups // lo, members // halves
    rows = residual.shape[0]

    def swap(value, x=0, z=0, y=0, c=0):
        flip = (z * lo + x) * members + y * halves + c
        return lax.ppermute(value, ("dp", "expert"), [(i, i ^ flip) for i in range(groups * members)])

    attended, w_gate = attend_local(
        queries, fresh_key, fresh_value, cached_keys, cached_values, lengths, sink_logit_rows, w_gate_up
    )
    blocks = [attended]
    for r in range(1, members):
        blocks.append(swap(attended, y=r // halves, c=r % halves))
    o_weight = bring(attended, o_weight)
    stream = project(blocks, o_weight, residual)

    others = [(x, y) for x in range(lo) for y in range(ys)][1:]
    line = jnp.concatenate([stream] + [swap(stream, z=z) for z in range(1, zs)], axis=0)
    near = [line] + [swap(line, x=x, y=y) for x, y in others]
    far = [swap(block, c=1) for block in near]
    keep, send = expert_sums(near, far, norm_gain, expert_ids, route_weights, w_gate, w_gate_up, w_down, groups, lo)

    def added(parts):
        total = parts[0].astype(jnp.float32)
        for part in parts[1:]:
            total = total + part.astype(jnp.float32)
        return total

    def cut(value, i):
        return value[i * rows:(i + 1) * rows]

    chip = [added([keep[i], swap(send[i], c=1)]).astype(jnp.bfloat16) for i in range(3)]
    last, _ = lax.optimization_barrier((send[3], chip[1]))
    chip.append(added([keep[3], swap(last, c=1)]).astype(jnp.bfloat16))
    plane = added([chip[0], swap(chip[1], y=1), swap(chip[2], x=1)]).astype(jnp.bfloat16)
    corner = added([cut(chip[3], 0)] + [swap(cut(chip[3], z), z=z) for z in range(1, zs)]).astype(jnp.bfloat16)
    total = added([stream, cut(plane, 0)] + [swap(cut(plane, z), z=z) for z in range(1, zs)] + [swap(corner, x=1, y=1)])
    return total.astype(jnp.bfloat16)


def attend(queries, fresh_key, fresh_value, cached_keys, cached_values, lengths, sink_logit_rows):
    batch_count = queries.shape[0]
    head_groups = QUERY_HEADS // KEY_VALUE_HEADS
    query_head_rows = queries.reshape(batch_count, KEY_VALUE_HEADS, head_groups, HEAD_SIZE)
    key_rows = cached_keys.reshape(batch_count, WINDOW_LENGTH, KEY_VALUE_HEADS, HEAD_SIZE)
    value_rows = cached_values.reshape(batch_count, WINDOW_LENGTH, KEY_VALUE_HEADS, HEAD_SIZE)
    score_scale = 1.0 / math.sqrt(HEAD_SIZE)
    cache_scores = (
        jnp.einsum("bkgd,bwkd->bkgw", query_head_rows, key_rows, preferred_element_type=jnp.float32)
        * score_scale
    )
    own_scores = (
        jnp.einsum(
            "npwm,npm->npw",
            query_head_rows,
            fresh_key.reshape(batch_count, KEY_VALUE_HEADS, HEAD_SIZE),
            preferred_element_type=jnp.float32,
        )
        * score_scale
    )
    slots = jnp.arange(WINDOW_LENGTH, dtype=jnp.int32)
    valid = (slots[None, :] >= (WINDOW_LENGTH - lengths)[:, None])[:, None, None, :]
    sink_terms = sink_logit_rows.reshape(KEY_VALUE_HEADS, head_groups)[None]
    masked = jnp.where(valid, cache_scores, -jnp.inf)
    top = jnp.maximum(jnp.maximum(jnp.max(masked, axis=-1), own_scores), sink_terms)
    cache_exp = jnp.where(valid, jnp.exp(masked - top[..., None]), 0.0)
    self_exp = jnp.exp(own_scores - top)
    total = jnp.sum(cache_exp, axis=-1) + self_exp + jnp.exp(sink_terms - top)
    cache_prob = (cache_exp / total[..., None]).astype(jnp.bfloat16)
    own_probability = (self_exp / total).astype(jnp.bfloat16)
    blended = jnp.einsum(
        "bkgw,bwkd->bkgd", cache_prob, value_rows, preferred_element_type=jnp.float32
    )
    blended = blended + own_probability.astype(jnp.float32)[..., None] * fresh_value.reshape(
        batch_count, KEY_VALUE_HEADS, 1, HEAD_SIZE
    ).astype(jnp.float32)
    return blended.reshape(batch_count, QUERY_HEADS * HEAD_SIZE).astype(jnp.bfloat16)


def slot_onehot(named, capacity):
    counts = jnp.cumsum(named.astype(jnp.int32), axis=1) - 1
    places = jnp.arange(capacity, dtype=jnp.int32)
    return named[:, None, :] & (counts[:, None, :] == places[None, :, None])


def receiver_slots(expert_ids, route_weights, expert, blocks, capacity):
    picked = expert_ids == expert
    named = jnp.any(picked, axis=1).reshape(blocks, -1)
    weight_at = jnp.sum(jnp.where(picked, route_weights, 0.0), axis=1).reshape(blocks, -1)
    onehot = slot_onehot(named, capacity)
    slot_weight = jnp.sum(jnp.where(onehot, weight_at[:, None, :], 0.0), axis=2)
    return (onehot, slot_weight)


def sender_slots(my_ids, experts, capacity):
    labels = jnp.arange(experts, dtype=jnp.int32)
    named = jnp.any(my_ids[None, :, :] == labels[:, None, None], axis=2)
    return slot_onehot(named, capacity)


def body(
    queries,
    fresh_key,
    fresh_value,
    cached_keys,
    cached_values,
    lengths,
    sink_logit_rows,
    residual,
    o_weight,
    norm_gain,
    expert_ids,
    route_weights,
    w_gate_up,
    w_down,
):
    attended = attend(
        queries, fresh_key, fresh_value, cached_keys, cached_values, lengths, sink_logit_rows
    )
    projected = lax.dot_general(
        lax.all_gather(attended, "expert", axis=0, tiled=True),
        o_weight,
        (((1,), (1,)), ((), ())),
        preferred_element_type=jnp.float32,
    )
    stream = (residual.astype(jnp.float32) + projected).astype(jnp.bfloat16)
    wide = stream.astype(jnp.float32)
    group_rows = stream.shape[0]
    columns = stream.shape[1]
    experts = lax.axis_size("dp")
    capacity = 2 * group_rows * TOP // experts
    gain_cols = lax.dynamic_slice_in_dim(norm_gain, lax.axis_index("expert") * columns, columns)
    squares = lax.psum(jnp.sum(wide * wide, axis=1), "expert")
    score_scale = lax.rsqrt(squares / D + norm_eps)
    outgoing = (wide * score_scale[:, None] * gain_cols[None, :]).astype(jnp.bfloat16)
    _, slot_weight = receiver_slots(
        expert_ids, route_weights, lax.axis_index("dp"), experts, capacity
    )
    my_ids = lax.dynamic_slice_in_dim(expert_ids, lax.axis_index("dp") * group_rows, group_rows, 0)
    onehot_out = sender_slots(my_ids, experts, capacity)
    outbound = jnp.einsum(
        "ect,td->ecd", onehot_out.astype(jnp.bfloat16), outgoing, preferred_element_type=jnp.float32
    ).astype(jnp.bfloat16)
    received = lax.all_to_all(outbound, "dp", split_axis=0, concat_axis=0, tiled=True)
    rows = received.reshape(experts * capacity, columns)
    gate_up = w_gate_up[0]
    down = w_down[0]
    both = jnp.einsum(
        "rc,hfc->rhf",
        lax.all_gather(rows, "expert", axis=1, tiled=True),
        gate_up,
        preferred_element_type=jnp.float32,
    )
    gate = both[:, 0]
    up = both[:, 1]
    hidden = ((up + 1.0) * gate * jax.nn.sigmoid(swish_alpha * gate)).astype(jnp.bfloat16)
    summed = lax.psum_scatter(
        lax.dot_general(
            down, hidden, (((0,), (1,)), ((), ())), preferred_element_type=jnp.float32
        ).astype(jnp.bfloat16),
        "expert",
        scatter_dimension=0,
        tiled=True,
    ).astype(jnp.float32)
    contribution = (summed * slot_weight.reshape(1, -1)).astype(jnp.bfloat16)
    contribution = contribution.T.reshape(experts, capacity, columns)
    returned = lax.all_to_all(contribution, "dp", split_axis=0, concat_axis=0, tiled=True)
    returned_sum = jnp.einsum(
        "ect,ecd->td",
        onehot_out.astype(jnp.float32),
        returned.astype(jnp.float32),
        precision=lax.Precision.HIGHEST,
    )
    return (wide + returned_sum).astype(jnp.bfloat16)


def solution(mesh):
    placed = (
        P(("dp", "expert"), None),
        P(("dp", "expert"), None),
        P(("dp", "expert"), None),
        P(("dp", "expert"), None, None),
        P(("dp", "expert"), None, None),
        P(("dp", "expert")),
        P(),
        P("dp", "expert"),
        P("expert", None),
        P(),
        P(),
        P(),
        P("dp", None, "expert", None),
        P("dp", "expert", None),
    )

    def layer(*args):
        group_rows = args[7].shape[0]
        groups, members = mesh.shape["dp"], mesh.shape["expert"]
        capacity = 2 * group_rows * TOP // groups
        paired = groups & (groups - 1) == 0 and groups > 1 and members == 4
        return (dense_body if capacity >= group_rows and paired else body)(*args)

    return jax.shard_map(
        layer, mesh=mesh, in_specs=placed, out_specs=P("dp", "expert"), check_vma=False
    )
```

profile of v0, /device:TPU:0, one launch (start us, length us, event | category | flops | bytes accessed | tf_op | source)
XLA Modules:
  0.0 57.5 jit_solution(16482737620372129945)
XLA Ops:
  0.0 2.6 %attend.1 = (bf16[8,2048]{1,0:T(8,128)(2,1)S(1)}, bf16[1,720,2880]{2,1,0:T(8,128)(2,1)S(1)}) custom-call(s32[8]{0:T(128)} %len_hbm.1, f32[32]{0:T(128)} %sink_hbm.1, bf16[8,2048]{1,0:T(8,128)(2,1)} %q_hbm.1, bf16[8,256]{1,0:T(8,128)(2,1)} %fk_hbm.1, bf16[8,256]{1,0:T(8,128)(2,1)} %fv_hbm.1, bf16[8,128,256]{2,1,0:T(8,128)(2,1)} %ck_hbm.1, ...), custom_call_target="tpu_custom_call" | custom-call | tf_op jit(solution)/shard_map/attend/pallas_call | solution.py:109
  2.7 0.0 copy-start
  2.7 0.0 copy-start.3
  2.7 0.0 copy-start.1
  2.7 0.0 copy-start.2
  2.7 2.5 %collective-permute-start.2 = (bf16[8,2048]{1,0:T(8,128)(2,1)S(1)}, bf16[8,2048]{1,0:T(8,128)(2,1)S(1)}, u32[]{:S(2)}, u32[]{:S(2)}) collective-permute-start(bf16[8,2048]{1,0:T(8,128)(2,1)S(1)} %get-tuple-element.16.after_ref.refs_0_), channel_id=1, source_target_pairs={{0,3},{1,2},{2,1},{3,0},{4,7},{5,6},{6,5},{7,4},{8,11},{9,10},{10,... | collective-permute-start | bytes 98312 | tf_op jit(solution)/shard_map/ppermute | solution.py:288
  5.2 0.6 %collective-permute-start.1 = (bf16[8,2048]{1,0:T(8,128)(2,1)S(1)}, bf16[8,2048]{1,0:T(8,128)(2,1)S(1)}, u32[]{:S(2)}, u32[]{:S(2)}) collective-permute-start(bf16[8,2048]{1,0:T(8,128)(2,1)S(1)} %get-tuple-element.16.after_ref.refs_0_), channel_id=1, source_target_pairs={{0,2},{1,3},{2,0},{3,1},{4,6},{5,7},{6,4},{7,5},{8,10},{9,11},{10,... | collective-permute-start | bytes 98312 | tf_op jit(solution)/shard_map/ppermute | solution.py:288
  5.8 0.0 collective-permute-start
  5.9 1.8 %bring.1.refs_4_ = bf16[720,2048]{1,0:T(8,128)(2,1)S(1)} custom-call(bf16[8,2048]{1,0:T(8,128)(2,1)S(1)} %get-tuple-element.16.after_ref.refs_0_, bf16[720,2048]{1,0:T(8,128)(2,1)} %source_hbm.1), custom_call_target="tpu_custom_call" | custom-call | flops 1000000000 | bytes 4194304 | tf_op jit(solution)/shard_map/bring/pallas_call | solution.py:144
  7.7 1.4 %collective-permute-done.1.refs_2_ = bf16[8,2048]{1,0:T(8,128)(2,1)S(1)} collective-permute-done((bf16[8,2048]{1,0:T(8,128)(2,1)S(1)}, bf16[8,2048]{1,0:T(8,128)(2,1)S(1)}, u32[]{:S(2)}, u32[]{:S(2)}) %collective-permute-start.1) | collective-permute-done | bytes 32800 | tf_op jit(solution)/shard_map/ppermute | solution.py:288
  9.2 0.0 collective-permute-done.refs_1_
  9.2 0.9 %project.1 = bf16[32,720]{1,0:T(8,128)(2,1)S(1)} custom-call(bf16[8,2048]{1,0:T(8,128)(2,1)S(1)} %get-tuple-element.16.after_ref.refs_0_, bf16[8,2048]{1,0:T(8,128)(2,1)S(1)} %collective-permute-done.refs_1_, bf16[8,2048]{1,0:T(8,128)(2,1)S(1)} %collective-permute-done.1.refs_2_, bf16[8,2048]{1,0:T(8,128)(2,1)S(1)} %collective-permute-done.2.refs_3_, ...), custom_call_target="tpu_custom_call" | custom-call | tf_op jit(solution)/shard_map/project/pallas_call | solution.py:161
  10.1 3.7 %collective-permute-start.5 = (bf16[32,720]{1,0:T(8,128)(2,1)S(1)}, bf16[32,720]{1,0:T(8,128)(2,1)S(1)}, u32[]{:S(2)}, u32[]{:S(2)}) collective-permute-start(bf16[32,720]{1,0:T(8,128)(2,1)S(1)} %project.1), channel_id=1, source_target_pairs={{0,24},{1,25},{2,26},{3,27},{4,28},{5,29},{6,30},{7,31},{8,16},{9,... | collective-permute-start | bytes 138248 | tf_op jit(solution)/shard_map/ppermute | solution.py:288
  13.8 0.8 %collective-permute-start.3 = (bf16[32,720]{1,0:T(8,128)(2,1)S(1)}, bf16[32,720]{1,0:T(8,128)(2,1)S(1)}, u32[]{:S(2)}, u32[]{:S(2)}) collective-permute-start(bf16[32,720]{1,0:T(8,128)(2,1)S(1)} %project.1), channel_id=1, source_target_pairs={{0,8},{1,9},{2,10},{3,11},{4,12},{5,13},{6,14},{7,15},{8,0},{9,1},... | collective-permute-start | bytes 138248 | tf_op jit(solution)/shard_map/ppermute | solution.py:288
  14.6 1.8 %collective-permute-done.5 = bf16[32,720]{1,0:T(8,128)(2,1)S(1)} collective-permute-done((bf16[32,720]{1,0:T(8,128)(2,1)S(1)}, bf16[32,720]{1,0:T(8,128)(2,1)S(1)}, u32[]{:S(2)}, u32[]{:S(2)}) %collective-permute-start.5) | collective-permute-done | bytes 46112 | tf_op jit(solution)/shard_map/ppermute | solution.py:288
  16.3 2.4 %collective-permute-done.4 = bf16[32,720]{1,0:T(8,128)(2,1)S(1)} collective-permute-done((bf16[32,720]{1,0:T(8,128)(2,1)S(1)}, bf16[32,720]{1,0:T(8,128)(2,1)S(1)}, u32[]{:S(2)}, u32[]{:S(2)}) %collective-permute-start.4) | collective-permute-done | bytes 46112 | tf_op jit(solution)/shard_map/ppermute | solution.py:288
  18.8 2.0 %collective-permute-start.8 = (bf16[128,720]{1,0:T(8,128)(2,1)S(1)}, bf16[128,720]{1,0:T(8,128)(2,1)S(1)}, u32[]{:S(2)}, u32[]{:S(2)}) collective-permute-start(bf16[128,720]{1,0:T(8,128)(2,1)S(1)} %pad_maximum_fusion.refs_0_), channel_id=1, source_target_pairs={{0,6},{1,7},{2,4},{3,5},{4,2},{5,3},{6,0},{7,1},{8,14},{9,15},{10,... | collective-permute-start | bytes 552968 | tf_op jit(solution)/shard_map/ppermute | solution.py:288
  20.8 0.5 collective-permute-start.7
  21.3 1.0 %collective-permute-start.6 = (bf16[128,720]{1,0:T(8,128)(2,1)S(1)}, bf16[128,720]{1,0:T(8,128)(2,1)S(1)}, u32[]{:S(2)}, u32[]{:S(2)}) collective-permute-start(bf16[128,720]{1,0:T(8,128)(2,1)S(1)} %pad_maximum_fusion.refs_0_), channel_id=1, source_target_pairs={{0,2},{1,3},{2,0},{3,1},{4,6},{5,7},{6,4},{7,5},{8,10},{9,11},{10,... | collective-permute-start | bytes 552968 | tf_op jit(solution)/shard_map/ppermute | solution.py:288
  22.3 5.2 %collective-permute-done.8.refs_3_ = bf16[128,720]{1,0:T(8,128)(2,1)S(1)} collective-permute-done((bf16[128,720]{1,0:T(8,128)(2,1)S(1)}, bf16[128,720]{1,0:T(8,128)(2,1)S(1)}, u32[]{:S(2)}, u32[]{:S(2)}) %collective-permute-start.8) | collective-permute-done | bytes 184352 | tf_op jit(solution)/shard_map/ppermute | solution.py:288
  27.5 2.0 %collective-permute-done.7.refs_2_ = bf16[128,720]{1,0:T(8,128)(2,1)S(1)} collective-permute-done((bf16[128,720]{1,0:T(8,128)(2,1)S(1)}, bf16[128,720]{1,0:T(8,128)(2,1)S(1)}, u32[]{:S(2)}, u32[]{:S(2)}) %collective-permute-start.7) | collective-permute-done | bytes 184352 | tf_op jit(solution)/shard_map/ppermute | solution.py:288
  29.5 0.2 collective-permute-done.6.refs_1_
  29.7 0.3 collective-permute-start.10
  30.1 0.9 %collective-permute-done.11.refs_6_ = bf16[128,720]{1,0:T(8,128)(2,1)S(1)} collective-permute-done((bf16[128,720]{1,0:T(8,128)(2,1)S(1)}, bf16[128,720]{1,0:T(8,128)(2,1)S(1)}, u32[]{:S(2)}, u32[]{:S(2)}) %collective-permute-start.11) | collective-permute-done | bytes 184352 | tf_op jit(solution)/shard_map/ppermute | solution.py:288
  31.0 0.3 collective-permute-done.10.refs_5_
  31.2 6.6 %experts.1 = (bf16[128,720]{1,0:T(8,128)(2,1)S(1)}, bf16[128,720]{1,0:T(8,128)(2,1)S(1)}, bf16[128,720]{1,0:T(8,128)(2,1)S(1)}, bf16[128,720]{1,0:T(8,128)(2,1)S...) custom-call(bf16[128,720]{1,0:T(8,128)(2,1)S(1)} %pad_maximum_fusion, ...), custom_call_target="tpu_custom_call" | custom-call | tf_op jit(solution)/shard_map/experts/pallas_call | solution.py:254
  37.8 0.3 collective-permute-start.14
  38.1 0.3 collective-permute-start.13
  38.4 0.2 collective-permute-start.16
  38.6 0.7 %collective-permute-done.14 = bf16[128,720]{1,0:T(8,128)(2,1)S(1)} collective-permute-done((bf16[128,720]{1,0:T(8,128)(2,1)S(1)}, bf16[128,720]{1,0:T(8,128)(2,1)S(1)}, u32[]{:S(2)}, u32[]{:S(2)}) %collective-permute-start.14) | collective-permute-done | bytes 184352 | tf_op jit(solution)/shard_map/ppermute | solution.py:288
  39.3 0.1 add_convert_fusion.3
  39.4 1.2 %collective-permute-start.15 = (bf16[128,720]{1,0:T(8,128)(2,1)S(1)}, bf16[128,720]{1,0:T(8,128)(2,1)S(1)}, u32[]{:S(2)}, u32[]{:S(2)}) collective-permute-start(bf16[128,720]{1,0:T(8,128)(2,1)S(1)} %add_convert_fusion.3), channel_id=1, source_target_pairs={{0,2},{1,3},{2,0},{3,1},{4,6},{5,7},{6,4},{7,5},{8,10},{9,11},{10,... | collective-permute-start | bytes 552968 | tf_op jit(solution)/shard_map/ppermute | solution.py:288
  40.6 0.1 add_convert_fusion.2
  40.7 1.6 %collective-permute-start.17 = (bf16[128,720]{1,0:T(8,128)(2,1)S(1)}, bf16[128,720]{1,0:T(8,128)(2,1)S(1)}, u32[]{:S(2)}, u32[]{:S(2)}) collective-permute-start(bf16[128,720]{1,0:T(8,128)(2,1)S(1)} %add_convert_fusion.2), channel_id=1, source_target_pairs={{0,4},{1,5},{2,6},{3,7},{4,0},{5,1},{6,2},{7,3},{8,12},{9,13},{10,... | collective-permute-start | bytes 552968 | tf_op jit(solution)/shard_map/ppermute | solution.py:288
  42.3 0.7 %collective-permute-start.22 = (bf16[32,720]{1,0:T(8,128)(2,1)S(1)}, bf16[32,720]{1,0:T(8,128)(2,1)S(1)}, u32[]{:S(2)}, u32[]{:S(2)}) collective-permute-start(bf16[32,720]{1,0:T(8,128)(2,1)S(1)} %get-tuple-element.30), channel_id=1, source_target_pairs={{0,8},{1,9},{2,10},{3,11},{4,12},{5,13},{6,14},{7,15},{8,0},{9,1},... | collective-permute-start | bytes 138248 | tf_op jit(solution)/shard_map/ppermute | solution.py:288
  43.0 2.4 %collective-permute-start.24 = (bf16[32,720]{1,0:T(8,128)(2,1)S(1)}, bf16[32,720]{1,0:T(8,128)(2,1)S(1)}, u32[]{:S(2)}, u32[]{:S(2)}) collective-permute-start(bf16[32,720]{1,0:T(8,128)(2,1)S(1)} %get-tuple-element.31), channel_id=1, source_target_pairs={{0,24},{1,25},{2,26},{3,27},{4,28},{5,29},{6,30},{7,31},{8,16},{9,... | collective-permute-start | bytes 138248 | tf_op jit(solution)/shard_map/ppermute | solution.py:288
  45.3 0.5 collective-permute-start.23
  45.9 0.6 %collective-permute-done.15 = bf16[128,720]{1,0:T(8,128)(2,1)S(1)} collective-permute-done((bf16[128,720]{1,0:T(8,128)(2,1)S(1)}, bf16[128,720]{1,0:T(8,128)(2,1)S(1)}, u32[]{:S(2)}, u32[]{:S(2)}) %collective-permute-start.15) | collective-permute-done | bytes 184352 | tf_op jit(solution)/shard_map/ppermute | solution.py:288
  46.5 1.6 %collective-permute-done.17 = bf16[128,720]{1,0:T(8,128)(2,1)S(1)} collective-permute-done((bf16[128,720]{1,0:T(8,128)(2,1)S(1)}, bf16[128,720]{1,0:T(8,128)(2,1)S(1)}, u32[]{:S(2)}, u32[]{:S(2)}) %collective-permute-start.17) | collective-permute-done | bytes 184352 | tf_op jit(solution)/shard_map/ppermute | solution.py:288
  48.1 0.1 add_convert_fusion.1
  48.2 0.7 %collective-permute-start.18 = (bf16[32,720]{1,0:T(8,128)(2,1)S(1)}, bf16[32,720]{1,0:T(8,128)(2,1)S(1)}, u32[]{:S(2)}, u32[]{:S(2)}) collective-permute-start(bf16[32,720]{1,0:T(8,128)(2,1)S(1)} %get-tuple-element.27), channel_id=1, source_target_pairs={{0,8},{1,9},{2,10},{3,11},{4,12},{5,13},{6,14},{7,15},{8,0},{9,1},... | collective-permute-start | bytes 138248 | tf_op jit(solution)/shard_map/ppermute | solution.py:288
  48.9 2.4 %collective-permute-start.20 = (bf16[32,720]{1,0:T(8,128)(2,1)S(1)}, bf16[32,720]{1,0:T(8,128)(2,1)S(1)}, u32[]{:S(2)}, u32[]{:S(2)}) collective-permute-start(bf16[32,720]{1,0:T(8,128)(2,1)S(1)} %get-tuple-element.28), channel_id=1, source_target_pairs={{0,24},{1,25},{2,26},{3,27},{4,28},{5,29},{6,30},{7,31},{8,16},{9,... | collective-permute-start | bytes 138248 | tf_op jit(solution)/shard_map/ppermute | solution.py:288
  51.2 0.5 collective-permute-start.19
  51.8 1.9 %collective-permute-start.25 = (bf16[32,720]{1,0:T(8,128)(2,1)S(1)}, bf16[32,720]{1,0:T(8,128)(2,1)S(1)}, u32[]{:S(2)}, u32[]{:S(2)}) collective-permute-start(bf16[32,720]{1,0:T(8,128)(2,1)S(1)} %add_convert_fusion.6), channel_id=1, source_target_pairs={{0,6},{1,7},{2,4},{3,5},{4,2},{5,3},{6,0},{7,1},{8,14},{9,15},{10,... | collective-permute-start | bytes 138248 | tf_op jit(solution)/shard_map/ppermute | solution.py:288
  53.7 1.2 %collective-permute-done.20 = bf16[32,720]{1,0:T(8,128)(2,1)S(1)} collective-permute-done((bf16[32,720]{1,0:T(8,128)(2,1)S(1)}, bf16[32,720]{1,0:T(8,128)(2,1)S(1)}, u32[]{:S(2)}, u32[]{:S(2)}) %collective-permute-start.20) | collective-permute-done | bytes 46112 | tf_op jit(solution)/shard_map/ppermute | solution.py:288
  54.8 1.7 %collective-permute-done.19 = bf16[32,720]{1,0:T(8,128)(2,1)S(1)} collective-permute-done((bf16[32,720]{1,0:T(8,128)(2,1)S(1)}, bf16[32,720]{1,0:T(8,128)(2,1)S(1)}, u32[]{:S(2)}, u32[]{:S(2)}) %collective-permute-start.19) | collective-permute-done | bytes 46112 | tf_op jit(solution)/shard_map/ppermute | solution.py:288
  56.6 0.3 collective-permute-done.25
  56.8 0.7 %add_convert_fusion.5 = bf16[32,720]{1,0:T(8,128)(2,1)} fusion(bf16[32,720]{1,0:T(8,128)(2,1)S(1)} %collective-permute-done.25, bf16[32,720]{1,0:T(8,128)(2,1)S(1)} %collective-permute-done.20, bf16[32,720]{1,0:T(8,128)(2,1)S(1)} %collective-permute-done.19, bf16[32,720]{1,0:T(8,128)(2,1)S(1)} %collective-permute-done.18, bf16[32,720]{1,0:T(8,128)(2,1)S(1)} %project.1, ...), kind=kLoop, calls=%fused_computation.6 | loop fusion | flops 276480 | bytes 322560 | tf_op jit(solution)/shard_map/convert_element_type | solution.py:320
  (26 shorter events, 0.2 us)
Async XLA Ops:
  2.7 6.5 %copy-start = (bf16[32,720]{1,0:T(8,128)(2,1)S(1)}, bf16[32,720]{1,0:T(8,128)(2,1)}, u32[]{:S(2)}) copy-start(bf16[32,720]{1,0:T(8,128)(2,1)} %refs_5_.1) | copy-start | bytes 138244
  2.7 27.4 %copy-start.3 = (f32[2880]{0:T(1024)S(1)}, f32[2880]{0:T(1024)}, u32[]{:S(2)}) copy-start(f32[2880]{0:T(1024)} %param.23) | copy-start | bytes 34564
  2.7 28.6 %copy-start.1 = (s32[256,4]{0,1:T(4,128)S(1)}, s32[256,4]{0,1:T(4,128)}, u32[]{:S(2)}) copy-start(s32[256,4]{0,1:T(4,128)} %param.24) | copy-start | bytes 12292
  2.7 28.6 %copy-start.2 = (f32[256,4]{0,1:T(4,128)S(1)}, f32[256,4]{0,1:T(4,128)}, u32[]{:S(2)}) copy-start(f32[256,4]{0,1:T(4,128)} %param.25) | copy-start | bytes 12292
  2.7 5.0 %collective-permute-start.2 = (bf16[8,2048]{1,0:T(8,128)(2,1)S(1)}, bf16[8,2048]{1,0:T(8,128)(2,1)S(1)}, u32[]{:S(2)}, u32[]{:S(2)}) collective-permute-start(bf16[8,2048]{1,0:T(8,128)(2,1)S(1)} %get-tuple-element.16.after_ref.refs_0_), channel_id=1, source_target_pairs={{0,3},{1,2},{2,1},{3,0},{4,7},{5,6},{6,5},{7,4},{8,11},{9,10},{10,... | collective-permute-start | bytes 98312 | tf_op jit(solution)/shard_map/ppermute | solution.py:288
  5.2 4.0 %collective-permute-start.1 = (bf16[8,2048]{1,0:T(8,128)(2,1)S(1)}, bf16[8,2048]{1,0:T(8,128)(2,1)S(1)}, u32[]{:S(2)}, u32[]{:S(2)}) collective-permute-start(bf16[8,2048]{1,0:T(8,128)(2,1)S(1)} %get-tuple-element.16.after_ref.refs_0_), channel_id=1, source_target_pairs={{0,2},{1,3},{2,0},{3,1},{4,6},{5,7},{6,4},{7,5},{8,10},{9,11},{10,... | collective-permute-start | bytes 98312 | tf_op jit(solution)/shard_map/ppermute | solution.py:288
  5.8 3.3 %collective-permute-start = (bf16[8,2048]{1,0:T(8,128)(2,1)S(1)}, bf16[8,2048]{1,0:T(8,128)(2,1)S(1)}, u32[]{:S(2)}, u32[]{:S(2)}) collective-permute-start(bf16[8,2048]{1,0:T(8,128)(2,1)S(1)} %get-tuple-element.16.after_ref.refs_0_), channel_id=1, source_target_pairs={{0,1},{1,0},{2,3},{3,2},{4,5},{5,4},{6,7},{7,6},{8,9},{9,8},{10,11... | collective-permute-start | bytes 98312 | tf_op jit(solution)/shard_map/ppermute | solution.py:288
  10.1 6.2 %collective-permute-start.5 = (bf16[32,720]{1,0:T(8,128)(2,1)S(1)}, bf16[32,720]{1,0:T(8,128)(2,1)S(1)}, u32[]{:S(2)}, u32[]{:S(2)}) collective-permute-start(bf16[32,720]{1,0:T(8,128)(2,1)S(1)} %project.1), channel_id=1, source_target_pairs={{0,24},{1,25},{2,26},{3,27},{4,28},{5,29},{6,30},{7,31},{8,16},{9,... | collective-permute-start | bytes 138248 | tf_op jit(solution)/shard_map/ppermute | solution.py:288
  13.8 5.0 %collective-permute-start.4 = (bf16[32,720]{1,0:T(8,128)(2,1)S(1)}, bf16[32,720]{1,0:T(8,128)(2,1)S(1)}, u32[]{:S(2)}, u32[]{:S(2)}) collective-permute-start(bf16[32,720]{1,0:T(8,128)(2,1)S(1)} %project.1), channel_id=1, source_target_pairs={{0,16},{1,17},{2,18},{3,19},{4,20},{5,21},{6,22},{7,23},{8,24},{9,... | collective-permute-start | bytes 138248 | tf_op jit(solution)/shard_map/ppermute | solution.py:288
  13.8 5.0 %collective-permute-start.3 = (bf16[32,720]{1,0:T(8,128)(2,1)S(1)}, bf16[32,720]{1,0:T(8,128)(2,1)S(1)}, u32[]{:S(2)}, u32[]{:S(2)}) collective-permute-start(bf16[32,720]{1,0:T(8,128)(2,1)S(1)} %project.1), channel_id=1, source_target_pairs={{0,8},{1,9},{2,10},{3,11},{4,12},{5,13},{6,14},{7,15},{8,0},{9,1},... | collective-permute-start | bytes 138248 | tf_op jit(solution)/shard_map/ppermute | solution.py:288
  18.8 8.7 %collective-permute-start.8 = (bf16[128,720]{1,0:T(8,128)(2,1)S(1)}, bf16[128,720]{1,0:T(8,128)(2,1)S(1)}, u32[]{:S(2)}, u32[]{:S(2)}) collective-permute-start(bf16[128,720]{1,0:T(8,128)(2,1)S(1)} %pad_maximum_fusion.refs_0_), channel_id=1, source_target_pairs={{0,6},{1,7},{2,4},{3,5},{4,2},{5,3},{6,0},{7,1},{8,14},{9,15},{10,... | collective-permute-start | bytes 552968 | tf_op jit(solution)/shard_map/ppermute | solution.py:288
  20.8 8.8 %collective-permute-start.7 = (bf16[128,720]{1,0:T(8,128)(2,1)S(1)}, bf16[128,720]{1,0:T(8,128)(2,1)S(1)}, u32[]{:S(2)}, u32[]{:S(2)}) collective-permute-start(bf16[128,720]{1,0:T(8,128)(2,1)S(1)} %pad_maximum_fusion.refs_0_), channel_id=1, source_target_pairs={{0,4},{1,5},{2,6},{3,7},{4,0},{5,1},{6,2},{7,3},{8,12},{9,13},{10,... | collective-permute-start | bytes 552968 | tf_op jit(solution)/shard_map/ppermute | solution.py:288
  21.3 8.4 %collective-permute-start.6 = (bf16[128,720]{1,0:T(8,128)(2,1)S(1)}, bf16[128,720]{1,0:T(8,128)(2,1)S(1)}, u32[]{:S(2)}, u32[]{:S(2)}) collective-permute-start(bf16[128,720]{1,0:T(8,128)(2,1)S(1)} %pad_maximum_fusion.refs_0_), channel_id=1, source_target_pairs={{0,2},{1,3},{2,0},{3,1},{4,6},{5,7},{6,4},{7,5},{8,10},{9,11},{10,... | collective-permute-start | bytes 552968 | tf_op jit(solution)/shard_map/ppermute | solution.py:288
  22.3 7.7 %collective-permute-start.9 = (bf16[128,720]{1,0:T(8,128)(2,1)S(1)}, bf16[128,720]{1,0:T(8,128)(2,1)S(1)}, u32[]{:S(2)}, u32[]{:S(2)}) collective-permute-start(bf16[128,720]{1,0:T(8,128)(2,1)S(1)} %pad_maximum_fusion.refs_0_), channel_id=1, source_target_pairs={{0,1},{1,0},{2,3},{3,2},{4,5},{5,4},{6,7},{7,6},{8,9},{9,8},{10,11... | collective-permute-start | bytes 552968 | tf_op jit(solution)/shard_map/ppermute | solution.py:288
  27.5 2.5 %collective-permute-start.12 = (bf16[128,720]{1,0:T(8,128)(2,1)S(1)}, bf16[128,720]{1,0:T(8,128)(2,1)S(1)}, u32[]{:S(2)}, u32[]{:S(2)}) collective-permute-start(bf16[128,720]{1,0:T(8,128)(2,1)S(1)} %collective-permute-done.8.refs_3_), channel_id=1, source_target_pairs={{0,1},{1,0},{2,3},{3,2},{4,5},{5,4},{6,7},{7,6},{8,9},{9,8},{10,11... | collective-permute-start | bytes 552968 | tf_op jit(solution)/shard_map/ppermute | solution.py:288
  29.5 1.4 %collective-permute-start.11 = (bf16[128,720]{1,0:T(8,128)(2,1)S(1)}, bf16[128,720]{1,0:T(8,128)(2,1)S(1)}, u32[]{:S(2)}, u32[]{:S(2)}) collective-permute-start(bf16[128,720]{1,0:T(8,128)(2,1)S(1)} %collective-permute-done.7.refs_2_), channel_id=1, source_target_pairs={{0,1},{1,0},{2,3},{3,2},{4,5},{5,4},{6,7},{7,6},{8,9},{9,8},{10,11... | collective-permute-start | bytes 552968 | tf_op jit(solution)/shard_map/ppermute | solution.py:288
  29.7 1.6 %collective-permute-start.10 = (bf16[128,720]{1,0:T(8,128)(2,1)S(1)}, bf16[128,720]{1,0:T(8,128)(2,1)S(1)}, u32[]{:S(2)}, u32[]{:S(2)}) collective-permute-start(bf16[128,720]{1,0:T(8,128)(2,1)S(1)} %collective-permute-done.6.refs_1_), channel_id=1, source_target_pairs={{0,1},{1,0},{2,3},{3,2},{4,5},{5,4},{6,7},{7,6},{8,9},{9,8},{10,11... | collective-permute-start | bytes 552968 | tf_op jit(solution)/shard_map/ppermute | solution.py:288
  37.8 1.5 %collective-permute-start.14 = (bf16[128,720]{1,0:T(8,128)(2,1)S(1)}, bf16[128,720]{1,0:T(8,128)(2,1)S(1)}, u32[]{:S(2)}, u32[]{:S(2)}) collective-permute-start(bf16[128,720]{1,0:T(8,128)(2,1)S(1)} %get-tuple-element.21), channel_id=1, source_target_pairs={{0,1},{1,0},{2,3},{3,2},{4,5},{5,4},{6,7},{7,6},{8,9},{9,8},{10,11... | collective-permute-start | bytes 552968 | tf_op jit(solution)/shard_map/ppermute | solution.py:288
  38.1 7.2 %collective-permute-start.13 = (bf16[128,720]{1,0:T(8,128)(2,1)S(1)}, bf16[128,720]{1,0:T(8,128)(2,1)S(1)}, u32[]{:S(2)}, u32[]{:S(2)}) collective-permute-start(bf16[128,720]{1,0:T(8,128)(2,1)S(1)} %get-tuple-element.19), channel_id=1, source_target_pairs={{0,1},{1,0},{2,3},{3,2},{4,5},{5,4},{6,7},{7,6},{8,9},{9,8},{10,11... | collective-permute-start | bytes 552968 | tf_op jit(solution)/shard_map/ppermute | solution.py:288
  38.4 2.2 %collective-permute-start.16 = (bf16[128,720]{1,0:T(8,128)(2,1)S(1)}, bf16[128,720]{1,0:T(8,128)(2,1)S(1)}, u32[]{:S(2)}, u32[]{:S(2)}) collective-permute-start(bf16[128,720]{1,0:T(8,128)(2,1)S(1)} %get-tuple-element.23), channel_id=1, source_target_pairs={{0,1},{1,0},{2,3},{3,2},{4,5},{5,4},{6,7},{7,6},{8,9},{9,8},{10,11... | collective-permute-start | bytes 552968 | tf_op jit(solution)/shard_map/ppermute | solution.py:288
  39.4 7.1 %collective-permute-start.15 = (bf16[128,720]{1,0:T(8,128)(2,1)S(1)}, bf16[128,720]{1,0:T(8,128)(2,1)S(1)}, u32[]{:S(2)}, u32[]{:S(2)}) collective-permute-start(bf16[128,720]{1,0:T(8,128)(2,1)S(1)} %add_convert_fusion.3), channel_id=1, source_target_pairs={{0,2},{1,3},{2,0},{3,1},{4,6},{5,7},{6,4},{7,5},{8,10},{9,11},{10,... | collective-permute-start | bytes 552968 | tf_op jit(solution)/shard_map/ppermute | solution.py:288
  40.6 1.6 %collective-permute-start.21 = (bf16[128,720]{1,0:T(8,128)(2,1)S(1)}, bf16[128,720]{1,0:T(8,128)(2,1)S(1)}, u32[]{:S(2)}, u32[]{:S(2)}) collective-permute-start(bf16[128,720]{1,0:T(8,128)(2,1)S(1)} %get-tuple-element.26), channel_id=1, source_target_pairs={{0,1},{1,0},{2,3},{3,2},{4,5},{5,4},{6,7},{7,6},{8,9},{9,8},{10,11... | collective-permute-start | bytes 552968 | tf_op jit(solution)/shard_map/ppermute | solution.py:288
  40.7 7.4 %collective-permute-start.17 = (bf16[128,720]{1,0:T(8,128)(2,1)S(1)}, bf16[128,720]{1,0:T(8,128)(2,1)S(1)}, u32[]{:S(2)}, u32[]{:S(2)}) collective-permute-start(bf16[128,720]{1,0:T(8,128)(2,1)S(1)} %add_convert_fusion.2), channel_id=1, source_target_pairs={{0,4},{1,5},{2,6},{3,7},{4,0},{5,1},{6,2},{7,3},{8,12},{9,13},{10,... | collective-permute-start | bytes 552968 | tf_op jit(solution)/shard_map/ppermute | solution.py:288
  42.3 8.9 %collective-permute-start.22 = (bf16[32,720]{1,0:T(8,128)(2,1)S(1)}, bf16[32,720]{1,0:T(8,128)(2,1)S(1)}, u32[]{:S(2)}, u32[]{:S(2)}) collective-permute-start(bf16[32,720]{1,0:T(8,128)(2,1)S(1)} %get-tuple-element.30), channel_id=1, source_target_pairs={{0,8},{1,9},{2,10},{3,11},{4,12},{5,13},{6,14},{7,15},{8,0},{9,1},... | collective-permute-start | bytes 138248 | tf_op jit(solution)/shard_map/ppermute | solution.py:288
  43.0 8.8 %collective-permute-start.24 = (bf16[32,720]{1,0:T(8,128)(2,1)S(1)}, bf16[32,720]{1,0:T(8,128)(2,1)S(1)}, u32[]{:S(2)}, u32[]{:S(2)}) collective-permute-start(bf16[32,720]{1,0:T(8,128)(2,1)S(1)} %get-tuple-element.31), channel_id=1, source_target_pairs={{0,24},{1,25},{2,26},{3,27},{4,28},{5,29},{6,30},{7,31},{8,16},{9,... | collective-permute-start | bytes 138248 | tf_op jit(solution)/shard_map/ppermute | solution.py:288
  45.3 6.4 %collective-permute-start.23 = (bf16[32,720]{1,0:T(8,128)(2,1)S(1)}, bf16[32,720]{1,0:T(8,128)(2,1)S(1)}, u32[]{:S(2)}, u32[]{:S(2)}) collective-permute-start(bf16[32,720]{1,0:T(8,128)(2,1)S(1)} %get-tuple-element.32), channel_id=1, source_target_pairs={{0,16},{1,17},{2,18},{3,19},{4,20},{5,21},{6,22},{7,23},{8,24},{9,... | collective-permute-start | bytes 138248 | tf_op jit(solution)/shard_map/ppermute | solution.py:288
  48.2 5.5 %collective-permute-start.18 = (bf16[32,720]{1,0:T(8,128)(2,1)S(1)}, bf16[32,720]{1,0:T(8,128)(2,1)S(1)}, u32[]{:S(2)}, u32[]{:S(2)}) collective-permute-start(bf16[32,720]{1,0:T(8,128)(2,1)S(1)} %get-tuple-element.27), channel_id=1, source_target_pairs={{0,8},{1,9},{2,10},{3,11},{4,12},{5,13},{6,14},{7,15},{8,0},{9,1},... | collective-permute-start | bytes 138248 | tf_op jit(solution)/shard_map/ppermute | solution.py:288
  48.9 6.0 %collective-permute-start.20 = (bf16[32,720]{1,0:T(8,128)(2,1)S(1)}, bf16[32,720]{1,0:T(8,128)(2,1)S(1)}, u32[]{:S(2)}, u32[]{:S(2)}) collective-permute-start(bf16[32,720]{1,0:T(8,128)(2,1)S(1)} %get-tuple-element.28), channel_id=1, source_target_pairs={{0,24},{1,25},{2,26},{3,27},{4,28},{5,29},{6,30},{7,31},{8,16},{9,... | collective-permute-start | bytes 138248 | tf_op jit(solution)/shard_map/ppermute | solution.py:288
  51.2 5.3 %collective-permute-start.19 = (bf16[32,720]{1,0:T(8,128)(2,1)S(1)}, bf16[32,720]{1,0:T(8,128)(2,1)S(1)}, u32[]{:S(2)}, u32[]{:S(2)}) collective-permute-start(bf16[32,720]{1,0:T(8,128)(2,1)S(1)} %get-tuple-element.29), channel_id=1, source_target_pairs={{0,16},{1,17},{2,18},{3,19},{4,20},{5,21},{6,22},{7,23},{8,24},{9,... | collective-permute-start | bytes 138248 | tf_op jit(solution)/shard_map/ppermute | solution.py:288
  51.8 5.1 %collective-permute-start.25 = (bf16[32,720]{1,0:T(8,128)(2,1)S(1)}, bf16[32,720]{1,0:T(8,128)(2,1)S(1)}, u32[]{:S(2)}, u32[]{:S(2)}) collective-permute-start(bf16[32,720]{1,0:T(8,128)(2,1)S(1)} %add_convert_fusion.6), channel_id=1, source_target_pairs={{0,6},{1,7},{2,4},{3,5},{4,2},{5,3},{6,0},{7,1},{8,14},{9,15},{10,... | collective-permute-start | bytes 138248 | tf_op jit(solution)/shard_map/ppermute | solution.py:288
where the time goes:
time: 57.7 us; the launch traced here: 57.5 us
  starting transfers between devices  24.1 us (42%)
  waiting for transfers between devices  20.3 us (35%)
  Pallas kernels  12 us (21%)
  other arithmetic  0.99 us (2%)
    ppermute x26, starting transfers between devices, swap(): lax.ppermute(value, ('dp', 'expert'), [(i, i ^ flip) for i in range(group...  24.1 us
    ppermute x26, waiting for transfers between devices, swap(): lax.ppermute(value, ('dp', 'expert'), [(i, i ^ flip) for i in range(group...  20.3 us
    pallas_call x1, Pallas kernels, expert_sums(): pl.pallas_call(functools.partial(expert_kernel, lo=lo, ys=ys), out_shape=...  6.56 us
    pallas_call x1, Pallas kernels, attend_local(): pl.pallas_call(attend_kernel, out_shape=[jax.ShapeDtypeStruct(shape, jnp....  2.64 us
    pallas_call x1, Pallas kernels, bring(): return call(after, weight)  1.84 us
  transfers between devices with their start and end apart: 26, of which 14 were waited for; matrix products, arithmetic and copies ran while one was open for 1% of the time, Pallas kernels for 3%

commit v1 on v0

--- a/solution.py
+++ b/solution.py
@@ -144,6 +144,32 @@
     return call(after, weight)
 
 
+def bring_experts_kernel(after_ref, gu_hbm, down_hbm, up_ref, down_ref, sem):
+    copies = [
+        pltpu.make_async_copy(gu_hbm.at[0, 1], up_ref, sem.at[0]),
+        pltpu.make_async_copy(down_hbm.at[0], down_ref, sem.at[1]),
+    ]
+    for copy in copies:
+        copy.start()
+    for copy in copies:
+        copy.wait()
+
+
+def bring_experts(after, w_gate_up, w_down):
+    call = pl.pallas_call(
+        bring_experts_kernel,
+        out_shape=[jax.ShapeDtypeStruct(w_down.shape[1:], w_down.dtype)] * 2,
+        in_specs=[VMEM, HBM, HBM],
+        out_specs=[VMEM] * 2,
+        scratch_shapes=[pltpu.SemaphoreType.DMA((2,))],
+        compiler_params=pltpu.CompilerParams(vmem_limit_bytes=12 * MIB),
+        cost_estimate=pl.CostEstimate(flops=10**9, bytes_accessed=8 * MIB, transcendentals=0),
+        name="bring_experts",
+    )
+    arrays = [in_hbm(w_gate_up), in_hbm(w_down)]
+    return call(after, *arrays)
+
+
 def project_kernel(*refs):
     blocks, (w_ref, res_ref, out_ref, rows_ref) = refs[:-4], refs[-4:]
     rows = blocks[0].shape[0]
@@ -172,21 +198,17 @@
 def expert_kernel(*refs, lo, ys):
     halves = 2
     pairs = lo * ys
-    near, far, (gain_ref, ids_ref, route_ref, gate_ref, gu_hbm, down_hbm) = (
+    near, far, (gain_ref, ids_ref, route_ref, gate_ref, up_ref, down_ref) = (
         refs[:pairs], refs[pairs:2 * pairs], refs[2 * pairs:2 * pairs + 6]
     )
     refs = refs[2 * pairs + 6:]
     keep, send = refs[:pairs], refs[pairs:2 * pairs]
-    x_ref, weight_ref, up_ref, down_ref, hidden_ref, sums_ref, sem = refs[2 * pairs:]
+    x_ref, weight_ref, hidden_ref, sums_ref = refs[2 * pairs:]
     span, columns = near[0].shape
     width = x_ref.shape[1]
     members = ys * halves
     group = lax.axis_index("dp")
     place = lax.axis_index("expert")
-    up_copy = pltpu.make_async_copy(gu_hbm.at[0, 1], up_ref, sem.at[0])
-    down_copy = pltpu.make_async_copy(down_hbm.at[0], down_ref, sem.at[1])
-    up_copy.start()
-    down_copy.start()
 
     groups = weight_ref.shape[0]
     tokens = ids_ref.shape[1]
@@ -222,10 +244,8 @@
     norm = jnp.concatenate(norms, axis=0)
     gate = gate * norm
     gate = gate * jax.nn.sigmoid(swish_alpha * gate)
-    up_copy.wait()
     up = lax.dot_general(x_all, up_ref[...], contract, preferred_element_type=jnp.float32)
     hidden_ref[...] = ((up * norm + 1.0) * gate).astype(jnp.bfloat16)
-    down_copy.wait()
     scale = jnp.concatenate([weight_ref[group ^ (z * lo + x)] for x in range(lo) for z in range(zs)], axis=0)
     hidden = hidden_ref[...]
     for i in range(0, width, 768):
@@ -245,8 +265,8 @@
                     ]
 
 
-def expert_sums(near, far, norm_gain, expert_ids, route_weights, w_gate, w_gate_up, w_down, groups, lo):
-    units, width = w_down.shape[1:]
+def expert_sums(near, far, norm_gain, expert_ids, route_weights, w_gate, w_up, w_down, groups, lo):
+    units, width = w_down.shape
     pairs = len(near)
     ys = pairs // lo
     span, columns = near[0].shape
@@ -254,21 +274,18 @@
     outs = pl.pallas_call(
         functools.partial(expert_kernel, lo=lo, ys=ys),
         out_shape=[jax.ShapeDtypeStruct((span, columns), jnp.bfloat16)] * (2 * pairs),
-        in_specs=[VMEM] * (2 * pairs + 4) + [HBM] * 2,
+        in_specs=[VMEM] * (2 * pairs + 6),
         out_specs=[VMEM] * (2 * pairs),
         scratch_shapes=[
             pltpu.VMEM((total, width), jnp.bfloat16),
             pltpu.VMEM((groups, total // groups, 1), jnp.float32),
-            pltpu.VMEM((units, width), jnp.bfloat16),
-            pltpu.VMEM((units, width), jnp.bfloat16),
             pltpu.VMEM((total, units), jnp.bfloat16),
             pltpu.VMEM((total, width), jnp.bfloat16),
-            pltpu.SemaphoreType.DMA((2,)),
         ],
-        compiler_params=pltpu.CompilerParams(vmem_limit_bytes=36 * MIB),
+        compiler_params=pltpu.CompilerParams(vmem_limit_bytes=24 * MIB),
         name="experts",
     )(
-        *near, *far, norm_gain[None, :], expert_ids.T, route_weights.T, w_gate, in_hbm(w_gate_up), in_hbm(w_down)
+        *near, *far, norm_gain[None, :], expert_ids.T, route_weights.T, w_gate, w_up, w_down
     )
     return outs[:pairs], outs[pairs:]
 
@@ -280,7 +297,7 @@
     groups = lax.axis_size("dp")
     members = lax.axis_size("expert")
     lo, halves = 2, 2
-    zs, ys = groups // lo, members // halves
+    zs = groups // lo
     rows = residual.shape[0]
 
     def swap(value, x=0, z=0, y=0, c=0):
@@ -296,11 +313,15 @@
     o_weight = bring(attended, o_weight)
     stream = project(blocks, o_weight, residual)
 
-    others = [(x, y) for x in range(lo) for y in range(ys)][1:]
+    corner = swap(stream, x=1, y=1)
     line = jnp.concatenate([stream] + [swap(stream, z=z) for z in range(1, zs)], axis=0)
-    near = [line] + [swap(line, x=x, y=y) for x, y in others]
+    spread = []
+    for z in range(1, zs):
+        spread.append(swap(corner, z=z))
+    w_up, w_down = bring_experts(line, w_gate_up, w_down)
+    near = [line, swap(line, y=1), swap(line, x=1), jnp.concatenate([corner] + spread, axis=0)]
     far = [swap(block, c=1) for block in near]
-    keep, send = expert_sums(near, far, norm_gain, expert_ids, route_weights, w_gate, w_gate_up, w_down, groups, lo)
+    keep, send = expert_sums(near, far, norm_gain, expert_ids, route_weights, w_gate, w_up, w_down, groups, lo)
 
     def added(parts):
         total = parts[0].astype(jnp.float32)

time: 57.7 us -> 62.5 us (1.083)
  starting transfers between devices: 24.1 us -> 27.9 us
  Pallas kernels: 12 us -> 14.3 us
  waiting for transfers between devices: 20.3 us -> 18.8 us
    ppermute x26 -> x29, starting transfers between devices: 24.1 us -> 27.9 us  [swap(): lax.ppermute(value, ('dp', 'expert'), [(i, i ^ flip) for i in range(group...]
    pallas_call x0 -> x1, Pallas kernels: none -> 3.52 us  [bring_experts(): return call(after, *arrays)]
    ppermute x26 -> x29, waiting for transfers between devices: 20.3 us -> 18.8 us  [swap(): lax.ppermute(value, ('dp', 'expert'), [(i, i ^ flip) for i in range(group...]
    pallas_call x1, Pallas kernels: 6.56 us -> 5.4 us  [expert_sums(): pl.pallas_call(functools.partial(expert_kernel, lo=lo, ys=ys), out_shape=...]
  transfers between devices with their start and end apart: 26 -> 29, of which waited for: 14 -> 11; matrix products, arithmetic and copies ran while one was open for 1% -> 1% of each run, Pallas kernels for 3% -> 9%
where the time goes in v1:
time: 62.5 us; the launch traced here: 62.4 us
  starting transfers between devices  27.9 us (45%)
  waiting for transfers between devices  18.8 us (30%)
  Pallas kernels  14.3 us (23%)
  other arithmetic  0.99 us (2%)
    ppermute x29, starting transfers between devices, swap(): lax.ppermute(value, ('dp', 'expert'), [(i, i ^ flip) for i in range(group...  27.9 us
    ppermute x29, waiting for transfers between devices, swap(): lax.ppermute(value, ('dp', 'expert'), [(i, i ^ flip) for i in range(group...  18.8 us
    pallas_call x1, Pallas kernels, expert_sums(): pl.pallas_call(functools.partial(expert_kernel, lo=lo, ys=ys), out_shape=...  5.4 us
    pallas_call x1, Pallas kernels, bring_experts(): return call(after, *arrays)  3.52 us
    pallas_call x1, Pallas kernels, attend_local(): pl.pallas_call(attend_kernel, out_shape=[jax.ShapeDtypeStruct(shape, jnp....  2.64 us
    pallas_call x1, Pallas kernels, bring(): return call(after, weight)  1.84 us
  transfers between devices with their start and end apart: 29, of which 11 were waited for; matrix products, arithmetic and copies ran while one was open for 1% of the time, Pallas kernels for 9%

profile of v1, /device:TPU:0, one launch (start us, length us, event | category | flops | bytes accessed | tf_op | source)
XLA Modules:
  0.0 62.4 jit_solution(5957928073586608317)
XLA Ops:
  0.0 2.6 %attend.1 = (bf16[8,2048]{1,0:T(8,128)(2,1)S(1)}, bf16[1,720,2880]{2,1,0:T(8,128)(2,1)S(1)}) custom-call(s32[8]{0:T(128)} %len_hbm.1, f32[32]{0:T(128)} %sink_hbm.1, bf16[8,2048]{1,0:T(8,128)(2,1)} %q_hbm.1, bf16[8,256]{1,0:T(8,128)(2,1)} %fk_hbm.1, bf16[8,256]{1,0:T(8,128)(2,1)} %fv_hbm.1, bf16[8,128,256]{2,1,0:T(8,128)(2,1)} %ck_hbm.1, ...), custom_call_target="tpu_custom_call" | custom-call | tf_op jit(solution)/shard_map/attend/pallas_call | solution.py:109
  2.7 2.5 %collective-permute-start.2 = (bf16[8,2048]{1,0:T(8,128)(2,1)S(1)}, bf16[8,2048]{1,0:T(8,128)(2,1)S(1)}, u32[]{:S(2)}, u32[]{:S(2)}) collective-permute-start(bf16[8,2048]{1,0:T(8,128)(2,1)S(1)} %get-tuple-element.18.after_ref.refs_0_), channel_id=1, source_target_pairs={{0,3},{1,2},{2,1},{3,0},{4,7},{5,6},{6,5},{7,4},{8,11},{9,10},{10,... | collective-permute-start | bytes 98312 | tf_op jit(solution)/shard_map/ppermute | solution.py:305
  5.2 0.6 %collective-permute-start.1 = (bf16[8,2048]{1,0:T(8,128)(2,1)S(1)}, bf16[8,2048]{1,0:T(8,128)(2,1)S(1)}, u32[]{:S(2)}, u32[]{:S(2)}) collective-permute-start(bf16[8,2048]{1,0:T(8,128)(2,1)S(1)} %get-tuple-element.18.after_ref.refs_0_), channel_id=1, source_target_pairs={{0,2},{1,3},{2,0},{3,1},{4,6},{5,7},{6,4},{7,5},{8,10},{9,11},{10,... | collective-permute-start | bytes 98312 | tf_op jit(solution)/shard_map/ppermute | solution.py:305
  5.8 0.0 collective-permute-start
  5.9 1.8 %bring.1.refs_4_ = bf16[720,2048]{1,0:T(8,128)(2,1)S(1)} custom-call(bf16[8,2048]{1,0:T(8,128)(2,1)S(1)} %get-tuple-element.18.after_ref.refs_0_, bf16[720,2048]{1,0:T(8,128)(2,1)} %source_hbm.1), custom_call_target="tpu_custom_call" | custom-call | flops 1000000000 | bytes 4194304 | tf_op jit(solution)/shard_map/bring/pallas_call | solution.py:144
  7.7 1.4 %collective-permute-done.1.refs_2_ = bf16[8,2048]{1,0:T(8,128)(2,1)S(1)} collective-permute-done((bf16[8,2048]{1,0:T(8,128)(2,1)S(1)}, bf16[8,2048]{1,0:T(8,128)(2,1)S(1)}, u32[]{:S(2)}, u32[]{:S(2)}) %collective-permute-start.1) | collective-permute-done | bytes 32800 | tf_op jit(solution)/shard_map/ppermute | solution.py:305
  9.2 0.9 %project.1 = bf16[32,720]{1,0:T(8,128)(2,1)S(1)} custom-call(bf16[8,2048]{1,0:T(8,128)(2,1)S(1)} %get-tuple-element.18.after_ref.refs_0_, bf16[8,2048]{1,0:T(8,128)(2,1)S(1)} %collective-permute-done.refs_1_, bf16[8,2048]{1,0:T(8,128)(2,1)S(1)} %collective-permute-done.1.refs_2_, bf16[8,2048]{1,0:T(8,128)(2,1)S(1)} %collective-permute-done.2.refs_3_, ...), custom_call_target="tpu_custom_call" | custom-call | tf_op jit(solution)/shard_map/project/pallas_call | solution.py:187
  10.1 3.7 %collective-permute-start.5 = (bf16[32,720]{1,0:T(8,128)(2,1)S(1)}, bf16[32,720]{1,0:T(8,128)(2,1)S(1)}, u32[]{:S(2)}, u32[]{:S(2)}) collective-permute-start(bf16[32,720]{1,0:T(8,128)(2,1)S(1)} %project.1), channel_id=1, source_target_pairs={{0,24},{1,25},{2,26},{3,27},{4,28},{5,29},{6,30},{7,31},{8,16},{9,... | collective-permute-start | bytes 138248 | tf_op jit(solution)/shard_map/ppermute | solution.py:305
  13.7 0.8 %collective-permute-start.3 = (bf16[32,720]{1,0:T(8,128)(2,1)S(1)}, bf16[32,720]{1,0:T(8,128)(2,1)S(1)}, u32[]{:S(2)}, u32[]{:S(2)}) collective-permute-start(bf16[32,720]{1,0:T(8,128)(2,1)S(1)} %project.1), channel_id=1, source_target_pairs={{0,8},{1,9},{2,10},{3,11},{4,12},{5,13},{6,14},{7,15},{8,0},{9,1},... | collective-permute-start | bytes 138248 | tf_op jit(solution)/shard_map/ppermute | solution.py:305
  14.5 1.9 %collective-permute-start.8 = (bf16[32,720]{1,0:T(8,128)(2,1)S(1)}, bf16[32,720]{1,0:T(8,128)(2,1)S(1)}, u32[]{:S(2)}, u32[]{:S(2)}) collective-permute-start(bf16[32,720]{1,0:T(8,128)(2,1)S(1)} %project.1), channel_id=1, source_target_pairs={{0,6},{1,7},{2,4},{3,5},{4,2},{5,3},{6,0},{7,1},{8,14},{9,15},{10,... | collective-permute-start | bytes 138248 | tf_op jit(solution)/shard_map/ppermute | solution.py:305
  16.4 2.3 %collective-permute-done.4 = bf16[32,720]{1,0:T(8,128)(2,1)S(1)} collective-permute-done((bf16[32,720]{1,0:T(8,128)(2,1)S(1)}, bf16[32,720]{1,0:T(8,128)(2,1)S(1)}, u32[]{:S(2)}, u32[]{:S(2)}) %collective-permute-start.4) | collective-permute-done | bytes 46112 | tf_op jit(solution)/shard_map/ppermute | solution.py:305
  18.8 0.1 collective-permute-start.12
  18.8 1.6 %collective-permute-start.7 = (bf16[128,720]{1,0:T(8,128)(2,1)S(1)}, bf16[128,720]{1,0:T(8,128)(2,1)S(1)}, u32[]{:S(2)}, u32[]{:S(2)}) collective-permute-start(bf16[128,720]{1,0:T(8,128)(2,1)S(1)} %pad_maximum_fusion.after_ref.refs_0_), channel_id=1, source_target_pairs={{0,4},{1,5},{2,6},{3,7},{4,0},{5,1},{6,2},{7,3},{8,12},{9,13},{10,... | collective-permute-start | bytes 552968 | tf_op jit(solution)/shard_map/ppermute | solution.py:305
  20.4 1.0 %collective-permute-start.6 = (bf16[128,720]{1,0:T(8,128)(2,1)S(1)}, bf16[128,720]{1,0:T(8,128)(2,1)S(1)}, u32[]{:S(2)}, u32[]{:S(2)}) collective-permute-start(bf16[128,720]{1,0:T(8,128)(2,1)S(1)} %pad_maximum_fusion.after_ref.refs_0_), channel_id=1, source_target_pairs={{0,2},{1,3},{2,0},{3,1},{4,6},{5,7},{6,4},{7,5},{8,10},{9,11},{10,... | collective-permute-start | bytes 552968 | tf_op jit(solution)/shard_map/ppermute | solution.py:305
  21.4 2.1 %collective-permute-start.11 = (bf16[32,720]{1,0:T(8,128)(2,1)S(1)}, bf16[32,720]{1,0:T(8,128)(2,1)S(1)}, u32[]{:S(2)}, u32[]{:S(2)}) collective-permute-start(bf16[32,720]{1,0:T(8,128)(2,1)S(1)} %collective-permute-done.8), channel_id=1, source_target_pairs={{0,24},{1,25},{2,26},{3,27},{4,28},{5,29},{6,30},{7,31},{8,16},{9,... | collective-permute-start | bytes 138248 | tf_op jit(solution)/shard_map/ppermute | solution.py:305
  23.5 0.4 collective-permute-start.9
  24.0 3.8 %collective-permute-done.9 = bf16[32,720]{1,0:T(8,128)(2,1)S(1)} collective-permute-done((bf16[32,720]{1,0:T(8,128)(2,1)S(1)}, bf16[32,720]{1,0:T(8,128)(2,1)S(1)}, u32[]{:S(2)}, u32[]{:S(2)}) %collective-permute-start.9) | collective-permute-done | bytes 46112 | tf_op jit(solution)/shard_map/ppermute | solution.py:305
  27.8 0.6 collective-permute-start.10
  28.4 4.7 %collective-permute-done.10 = bf16[32,720]{1,0:T(8,128)(2,1)S(1)} collective-permute-done((bf16[32,720]{1,0:T(8,128)(2,1)S(1)}, bf16[32,720]{1,0:T(8,128)(2,1)S(1)}, u32[]{:S(2)}, u32[]{:S(2)}) %collective-permute-start.10) | collective-permute-done | bytes 46112 | tf_op jit(solution)/shard_map/ppermute | solution.py:305
  33.1 0.1 collective-permute-start.15
  33.2 0.5 collective-permute-start.14
  33.7 0.1 collective-permute-start.13
  33.8 3.5 %bring_experts.1 = (bf16[720,2880]{1,0:T(8,128)(2,1)S(1)}, bf16[720,2880]{1,0:T(8,128)(2,1)S(1)}) custom-call(bf16[128,720]{1,0:T(8,128)(2,1)S(1)} %pad_maximum_fusion.after_ref.refs_0_, bf16[1,2,720,2880]{3,2,1,0:T(8,128)(2,1)} %gu_hbm.3, bf16[1,720,2880]{2,1,0:T(8,128)(2,1)} %down_hbm.1), custom_call_target="tpu_custom_call" | custom-call | flops 1000000000 | bytes 8388608 | tf_op jit(solution)/shard_map/bring_experts/pallas_call | solution.py:170
  37.4 5.4 %experts.1 = (bf16[128,720]{1,0:T(8,128)(2,1)S(1)}, bf16[128,720]{1,0:T(8,128)(2,1)S(1)}, bf16[128,720]{1,0:T(8,128)(2,1)S(1)}, bf16[128,720]{1,0:T(8,128)(2,1)S...) custom-call(bf16[128,720]{1,0:T(8,128)(2,1)S(1)} %pad_maximum_fusion, ...), custom_call_target="tpu_custom_call" | custom-call | tf_op jit(solution)/shard_map/experts/pallas_call | solution.py:274
  42.8 0.5 collective-permute-start.17
  43.3 0.1 collective-permute-start.16
  43.4 0.4 collective-permute-start.19
  43.8 0.6 collective-permute-done.17
  44.4 0.1 add_convert_fusion.3
  44.5 1.0 %collective-permute-start.18 = (bf16[128,720]{1,0:T(8,128)(2,1)S(1)}, bf16[128,720]{1,0:T(8,128)(2,1)S(1)}, u32[]{:S(2)}, u32[]{:S(2)}) collective-permute-start(bf16[128,720]{1,0:T(8,128)(2,1)S(1)} %add_convert_fusion.3), channel_id=1, source_target_pairs={{0,2},{1,3},{2,0},{3,1},{4,6},{5,7},{6,4},{7,5},{8,10},{9,11},{10,... | collective-permute-start | bytes 552968 | tf_op jit(solution)/shard_map/ppermute | solution.py:305
  45.5 0.1 collective-permute-start.24
  45.6 0.1 add_convert_fusion.2
  45.7 1.1 %collective-permute-start.20 = (bf16[128,720]{1,0:T(8,128)(2,1)S(1)}, bf16[128,720]{1,0:T(8,128)(2,1)S(1)}, u32[]{:S(2)}, u32[]{:S(2)}) collective-permute-start(bf16[128,720]{1,0:T(8,128)(2,1)S(1)} %add_convert_fusion.2), channel_id=1, source_target_pairs={{0,4},{1,5},{2,6},{3,7},{4,0},{5,1},{6,2},{7,3},{8,12},{9,13},{10,... | collective-permute-start | bytes 552968 | tf_op jit(solution)/shard_map/ppermute | solution.py:305
  46.8 0.1 collective-permute-done.24
  47.0 0.1 collective-permute-start.25
  47.1 1.8 %collective-permute-start.27 = (bf16[32,720]{1,0:T(8,128)(2,1)S(1)}, bf16[32,720]{1,0:T(8,128)(2,1)S(1)}, u32[]{:S(2)}, u32[]{:S(2)}) collective-permute-start(bf16[32,720]{1,0:T(8,128)(2,1)S(1)} %get-tuple-element.35), channel_id=1, source_target_pairs={{0,24},{1,25},{2,26},{3,27},{4,28},{5,29},{6,30},{7,31},{8,16},{9,... | collective-permute-start | bytes 138248 | tf_op jit(solution)/shard_map/ppermute | solution.py:305
  48.9 1.6 %collective-permute-start.26 = (bf16[32,720]{1,0:T(8,128)(2,1)S(1)}, bf16[32,720]{1,0:T(8,128)(2,1)S(1)}, u32[]{:S(2)}, u32[]{:S(2)}) collective-permute-start(bf16[32,720]{1,0:T(8,128)(2,1)S(1)} %get-tuple-element.36), channel_id=1, source_target_pairs={{0,16},{1,17},{2,18},{3,19},{4,20},{5,21},{6,22},{7,23},{8,24},{9,... | collective-permute-start | bytes 138248 | tf_op jit(solution)/shard_map/ppermute | solution.py:305
  50.6 1.1 %collective-permute-done.18 = bf16[128,720]{1,0:T(8,128)(2,1)S(1)} collective-permute-done((bf16[128,720]{1,0:T(8,128)(2,1)S(1)}, bf16[128,720]{1,0:T(8,128)(2,1)S(1)}, u32[]{:S(2)}, u32[]{:S(2)}) %collective-permute-start.18) | collective-permute-done | bytes 184352 | tf_op jit(solution)/shard_map/ppermute | solution.py:305
  51.7 1.2 %collective-permute-done.20 = bf16[128,720]{1,0:T(8,128)(2,1)S(1)} collective-permute-done((bf16[128,720]{1,0:T(8,128)(2,1)S(1)}, bf16[128,720]{1,0:T(8,128)(2,1)S(1)}, u32[]{:S(2)}, u32[]{:S(2)}) %collective-permute-start.20) | collective-permute-done | bytes 184352 | tf_op jit(solution)/shard_map/ppermute | solution.py:305
  52.9 0.1 add_convert_fusion.1
  53.1 0.1 collective-permute-start.21
  53.2 1.8 %collective-permute-start.23 = (bf16[32,720]{1,0:T(8,128)(2,1)S(1)}, bf16[32,720]{1,0:T(8,128)(2,1)S(1)}, u32[]{:S(2)}, u32[]{:S(2)}) collective-permute-start(bf16[32,720]{1,0:T(8,128)(2,1)S(1)} %get-tuple-element.32), channel_id=1, source_target_pairs={{0,24},{1,25},{2,26},{3,27},{4,28},{5,29},{6,30},{7,31},{8,16},{9,... | collective-permute-start | bytes 138248 | tf_op jit(solution)/shard_map/ppermute | solution.py:305
  55.0 1.6 %collective-permute-start.22 = (bf16[32,720]{1,0:T(8,128)(2,1)S(1)}, bf16[32,720]{1,0:T(8,128)(2,1)S(1)}, u32[]{:S(2)}, u32[]{:S(2)}) collective-permute-start(bf16[32,720]{1,0:T(8,128)(2,1)S(1)} %get-tuple-element.33), channel_id=1, source_target_pairs={{0,16},{1,17},{2,18},{3,19},{4,20},{5,21},{6,22},{7,23},{8,24},{9,... | collective-permute-start | bytes 138248 | tf_op jit(solution)/shard_map/ppermute | solution.py:305
  56.7 1.6 %collective-permute-start.28 = (bf16[32,720]{1,0:T(8,128)(2,1)S(1)}, bf16[32,720]{1,0:T(8,128)(2,1)S(1)}, u32[]{:S(2)}, u32[]{:S(2)}) collective-permute-start(bf16[32,720]{1,0:T(8,128)(2,1)S(1)} %add_convert_fusion.6), channel_id=1, source_target_pairs={{0,6},{1,7},{2,4},{3,5},{4,2},{5,3},{6,0},{7,1},{8,14},{9,15},{10,... | collective-permute-start | bytes 138248 | tf_op jit(solution)/shard_map/ppermute | solution.py:305
  58.3 0.8 %collective-permute-done.23 = bf16[32,720]{1,0:T(8,128)(2,1)S(1)} collective-permute-done((bf16[32,720]{1,0:T(8,128)(2,1)S(1)}, bf16[32,720]{1,0:T(8,128)(2,1)S(1)}, u32[]{:S(2)}, u32[]{:S(2)}) %collective-permute-start.23) | collective-permute-done | bytes 46112 | tf_op jit(solution)/shard_map/ppermute | solution.py:305
  59.1 1.8 %collective-permute-done.22 = bf16[32,720]{1,0:T(8,128)(2,1)S(1)} collective-permute-done((bf16[32,720]{1,0:T(8,128)(2,1)S(1)}, bf16[32,720]{1,0:T(8,128)(2,1)S(1)}, u32[]{:S(2)}, u32[]{:S(2)}) %collective-permute-start.22) | collective-permute-done | bytes 46112 | tf_op jit(solution)/shard_map/ppermute | solution.py:305
  60.9 0.8 %collective-permute-done.28 = bf16[32,720]{1,0:T(8,128)(2,1)S(1)} collective-permute-done((bf16[32,720]{1,0:T(8,128)(2,1)S(1)}, bf16[32,720]{1,0:T(8,128)(2,1)S(1)}, u32[]{:S(2)}, u32[]{:S(2)}) %collective-permute-start.28) | collective-permute-done | bytes 46112 | tf_op jit(solution)/shard_map/ppermute | solution.py:305
  61.7 0.7 %add_convert_fusion.5 = bf16[32,720]{1,0:T(8,128)(2,1)} fusion(bf16[32,720]{1,0:T(8,128)(2,1)S(1)} %collective-permute-done.28, bf16[32,720]{1,0:T(8,128)(2,1)S(1)} %collective-permute-done.23, bf16[32,720]{1,0:T(8,128)(2,1)S(1)} %collective-permute-done.22, bf16[32,720]{1,0:T(8,128)(2,1)S(1)} %collective-permute-done.21, bf16[32,720]{1,0:T(8,128)(2,1)S(1)} %project.1, ...), kind=kLoop, calls=%fused_computation.6 | loop fusion | flops 276480 | bytes 322560 | tf_op jit(solution)/shard_map/convert_element_type | solution.py:341
  (37 shorter events, 0.2 us)
Async XLA Ops:
  2.7 6.5 %copy-start = (bf16[32,720]{1,0:T(8,128)(2,1)S(1)}, bf16[32,720]{1,0:T(8,128)(2,1)}, u32[]{:S(2)}) copy-start(bf16[32,720]{1,0:T(8,128)(2,1)} %refs_5_.1) | copy-start | bytes 138244
  2.7 31.1 %copy-start.3 = (f32[2880]{0:T(1024)S(1)}, f32[2880]{0:T(1024)}, u32[]{:S(2)}) copy-start(f32[2880]{0:T(1024)} %param.23) | copy-start | bytes 34564
  2.7 5.0 %collective-permute-start.2 = (bf16[8,2048]{1,0:T(8,128)(2,1)S(1)}, bf16[8,2048]{1,0:T(8,128)(2,1)S(1)}, u32[]{:S(2)}, u32[]{:S(2)}) collective-permute-start(bf16[8,2048]{1,0:T(8,128)(2,1)S(1)} %get-tuple-element.18.after_ref.refs_0_), channel_id=1, source_target_pairs={{0,3},{1,2},{2,1},{3,0},{4,7},{5,6},{6,5},{7,4},{8,11},{9,10},{10,... | collective-permute-start | bytes 98312 | tf_op jit(solution)/shard_map/ppermute | solution.py:305
  5.2 4.0 %collective-permute-start.1 = (bf16[8,2048]{1,0:T(8,128)(2,1)S(1)}, bf16[8,2048]{1,0:T(8,128)(2,1)S(1)}, u32[]{:S(2)}, u32[]{:S(2)}) collective-permute-start(bf16[8,2048]{1,0:T(8,128)(2,1)S(1)} %get-tuple-element.18.after_ref.refs_0_), channel_id=1, source_target_pairs={{0,2},{1,3},{2,0},{3,1},{4,6},{5,7},{6,4},{7,5},{8,10},{9,11},{10,... | collective-permute-start | bytes 98312 | tf_op jit(solution)/shard_map/ppermute | solution.py:305
  5.8 3.3 %collective-permute-start = (bf16[8,2048]{1,0:T(8,128)(2,1)S(1)}, bf16[8,2048]{1,0:T(8,128)(2,1)S(1)}, u32[]{:S(2)}, u32[]{:S(2)}) collective-permute-start(bf16[8,2048]{1,0:T(8,128)(2,1)S(1)} %get-tuple-element.18.after_ref.refs_0_), channel_id=1, source_target_pairs={{0,1},{1,0},{2,3},{3,2},{4,5},{5,4},{6,7},{7,6},{8,9},{9,8},{10,11... | collective-permute-start | bytes 98312 | tf_op jit(solution)/shard_map/ppermute | solution.py:305
  10.1 6.4 %collective-permute-start.5 = (bf16[32,720]{1,0:T(8,128)(2,1)S(1)}, bf16[32,720]{1,0:T(8,128)(2,1)S(1)}, u32[]{:S(2)}, u32[]{:S(2)}) collective-permute-start(bf16[32,720]{1,0:T(8,128)(2,1)S(1)} %project.1), channel_id=1, source_target_pairs={{0,24},{1,25},{2,26},{3,27},{4,28},{5,29},{6,30},{7,31},{8,16},{9,... | collective-permute-start | bytes 138248 | tf_op jit(solution)/shard_map/ppermute | solution.py:305
  13.7 5.0 %collective-permute-start.4 = (bf16[32,720]{1,0:T(8,128)(2,1)S(1)}, bf16[32,720]{1,0:T(8,128)(2,1)S(1)}, u32[]{:S(2)}, u32[]{:S(2)}) collective-permute-start(bf16[32,720]{1,0:T(8,128)(2,1)S(1)} %project.1), channel_id=1, source_target_pairs={{0,16},{1,17},{2,18},{3,19},{4,20},{5,21},{6,22},{7,23},{8,24},{9,... | collective-permute-start | bytes 138248 | tf_op jit(solution)/shard_map/ppermute | solution.py:305
  13.7 5.0 %collective-permute-start.3 = (bf16[32,720]{1,0:T(8,128)(2,1)S(1)}, bf16[32,720]{1,0:T(8,128)(2,1)S(1)}, u32[]{:S(2)}, u32[]{:S(2)}) collective-permute-start(bf16[32,720]{1,0:T(8,128)(2,1)S(1)} %project.1), channel_id=1, source_target_pairs={{0,8},{1,9},{2,10},{3,11},{4,12},{5,13},{6,14},{7,15},{8,0},{9,1},... | collective-permute-start | bytes 138248 | tf_op jit(solution)/shard_map/ppermute | solution.py:305
  14.5 6.8 %collective-permute-start.8 = (bf16[32,720]{1,0:T(8,128)(2,1)S(1)}, bf16[32,720]{1,0:T(8,128)(2,1)S(1)}, u32[]{:S(2)}, u32[]{:S(2)}) collective-permute-start(bf16[32,720]{1,0:T(8,128)(2,1)S(1)} %project.1), channel_id=1, source_target_pairs={{0,6},{1,7},{2,4},{3,5},{4,2},{5,3},{6,0},{7,1},{8,14},{9,15},{10,... | collective-permute-start | bytes 138248 | tf_op jit(solution)/shard_map/ppermute | solution.py:305
  18.8 18.6 %collective-permute-start.12 = (bf16[128,720]{1,0:T(8,128)(2,1)S(1)}, bf16[128,720]{1,0:T(8,128)(2,1)S(1)}, u32[]{:S(2)}, u32[]{:S(2)}) collective-permute-start(bf16[128,720]{1,0:T(8,128)(2,1)S(1)} %pad_maximum_fusion.after_ref.refs_0_), channel_id=1, source_target_pairs={{0,1},{1,0},{2,3},{3,2},{4,5},{5,4},{6,7},{7,6},{8,9},{9,8},{10,11... | collective-permute-start | bytes 552968 | tf_op jit(solution)/shard_map/ppermute | solution.py:305
  18.8 14.4 %collective-permute-start.7 = (bf16[128,720]{1,0:T(8,128)(2,1)S(1)}, bf16[128,720]{1,0:T(8,128)(2,1)S(1)}, u32[]{:S(2)}, u32[]{:S(2)}) collective-permute-start(bf16[128,720]{1,0:T(8,128)(2,1)S(1)} %pad_maximum_fusion.after_ref.refs_0_), channel_id=1, source_target_pairs={{0,4},{1,5},{2,6},{3,7},{4,0},{5,1},{6,2},{7,3},{8,12},{9,13},{10,... | collective-permute-start | bytes 552968 | tf_op jit(solution)/shard_map/ppermute | solution.py:305
  20.4 13.3 %collective-permute-start.6 = (bf16[128,720]{1,0:T(8,128)(2,1)S(1)}, bf16[128,720]{1,0:T(8,128)(2,1)S(1)}, u32[]{:S(2)}, u32[]{:S(2)}) collective-permute-start(bf16[128,720]{1,0:T(8,128)(2,1)S(1)} %pad_maximum_fusion.after_ref.refs_0_), channel_id=1, source_target_pairs={{0,2},{1,3},{2,0},{3,1},{4,6},{5,7},{6,4},{7,5},{8,10},{9,11},{10,... | collective-permute-start | bytes 552968 | tf_op jit(solution)/shard_map/ppermute | solution.py:305
  21.4 11.7 %collective-permute-start.11 = (bf16[32,720]{1,0:T(8,128)(2,1)S(1)}, bf16[32,720]{1,0:T(8,128)(2,1)S(1)}, u32[]{:S(2)}, u32[]{:S(2)}) collective-permute-start(bf16[32,720]{1,0:T(8,128)(2,1)S(1)} %collective-permute-done.8), channel_id=1, source_target_pairs={{0,24},{1,25},{2,26},{3,27},{4,28},{5,29},{6,30},{7,31},{8,16},{9,... | collective-permute-start | bytes 138248 | tf_op jit(solution)/shard_map/ppermute | solution.py:305
  23.5 4.3 %collective-permute-start.9 = (bf16[32,720]{1,0:T(8,128)(2,1)S(1)}, bf16[32,720]{1,0:T(8,128)(2,1)S(1)}, u32[]{:S(2)}, u32[]{:S(2)}) collective-permute-start(bf16[32,720]{1,0:T(8,128)(2,1)S(1)} %collective-permute-done.8), channel_id=1, source_target_pairs={{0,8},{1,9},{2,10},{3,11},{4,12},{5,13},{6,14},{7,15},{8,0},{9,1},... | collective-permute-start | bytes 138248 | tf_op jit(solution)/shard_map/ppermute | solution.py:305
  27.8 5.3 %collective-permute-start.10 = (bf16[32,720]{1,0:T(8,128)(2,1)S(1)}, bf16[32,720]{1,0:T(8,128)(2,1)S(1)}, u32[]{:S(2)}, u32[]{:S(2)}) collective-permute-start(bf16[32,720]{1,0:T(8,128)(2,1)S(1)} %collective-permute-done.8), channel_id=1, source_target_pairs={{0,16},{1,17},{2,18},{3,19},{4,20},{5,21},{6,22},{7,23},{8,24},{9,... | collective-permute-start | bytes 138248 | tf_op jit(solution)/shard_map/ppermute | solution.py:305
  33.1 4.2 %collective-permute-start.15 = (bf16[128,720]{1,0:T(8,128)(2,1)S(1)}, bf16[128,720]{1,0:T(8,128)(2,1)S(1)}, u32[]{:S(2)}, u32[]{:S(2)}) collective-permute-start(bf16[128,720]{1,0:T(8,128)(2,1)S(1)} %constant_dynamic-update-slice_fusion.refs_3_), channel_id=1, source_target_pairs={{0,1},{1,0},{2,3},{3,2},{4,5},{5,4},{6,7},{7,6},{8,9},{9,8},{10,11... | collective-permute-start | bytes 552968 | tf_op jit(solution)/shard_map/ppermute | solution.py:305
  33.2 4.2 %collective-permute-start.14 = (bf16[128,720]{1,0:T(8,128)(2,1)S(1)}, bf16[128,720]{1,0:T(8,128)(2,1)S(1)}, u32[]{:S(2)}, u32[]{:S(2)}) collective-permute-start(bf16[128,720]{1,0:T(8,128)(2,1)S(1)} %collective-permute-done.7.refs_2_), channel_id=1, source_target_pairs={{0,1},{1,0},{2,3},{3,2},{4,5},{5,4},{6,7},{7,6},{8,9},{9,8},{10,11... | collective-permute-start | bytes 552968 | tf_op jit(solution)/shard_map/ppermute | solution.py:305
  33.7 3.7 %collective-permute-start.13 = (bf16[128,720]{1,0:T(8,128)(2,1)S(1)}, bf16[128,720]{1,0:T(8,128)(2,1)S(1)}, u32[]{:S(2)}, u32[]{:S(2)}) collective-permute-start(bf16[128,720]{1,0:T(8,128)(2,1)S(1)} %collective-permute-done.6.refs_1_), channel_id=1, source_target_pairs={{0,1},{1,0},{2,3},{3,2},{4,5},{5,4},{6,7},{7,6},{8,9},{9,8},{10,11... | collective-permute-start | bytes 552968 | tf_op jit(solution)/shard_map/ppermute | solution.py:305
  33.8 3.6 %copy-start.1 = (s32[256,4]{0,1:T(4,128)S(1)}, s32[256,4]{0,1:T(4,128)}, u32[]{:S(2)}) copy-start(s32[256,4]{0,1:T(4,128)} %param.24) | copy-start | bytes 12292
  33.8 3.6 %copy-start.2 = (f32[256,4]{0,1:T(4,128)S(1)}, f32[256,4]{0,1:T(4,128)}, u32[]{:S(2)}) copy-start(f32[256,4]{0,1:T(4,128)} %param.25) | copy-start | bytes 12292
  42.8 1.6 %collective-permute-start.17 = (bf16[128,720]{1,0:T(8,128)(2,1)S(1)}, bf16[128,720]{1,0:T(8,128)(2,1)S(1)}, u32[]{:S(2)}, u32[]{:S(2)}) collective-permute-start(bf16[128,720]{1,0:T(8,128)(2,1)S(1)} %get-tuple-element.25), channel_id=1, source_target_pairs={{0,1},{1,0},{2,3},{3,2},{4,5},{5,4},{6,7},{7,6},{8,9},{9,8},{10,11... | collective-permute-start | bytes 552968 | tf_op jit(solution)/shard_map/ppermute | solution.py:305
  43.3 5.6 %collective-permute-start.16 = (bf16[128,720]{1,0:T(8,128)(2,1)S(1)}, bf16[128,720]{1,0:T(8,128)(2,1)S(1)}, u32[]{:S(2)}, u32[]{:S(2)}) collective-permute-start(bf16[128,720]{1,0:T(8,128)(2,1)S(1)} %get-tuple-element.23), channel_id=1, source_target_pairs={{0,1},{1,0},{2,3},{3,2},{4,5},{5,4},{6,7},{7,6},{8,9},{9,8},{10,11... | collective-permute-start | bytes 552968 | tf_op jit(solution)/shard_map/ppermute | solution.py:305
  43.4 2.2 %collective-permute-start.19 = (bf16[128,720]{1,0:T(8,128)(2,1)S(1)}, bf16[128,720]{1,0:T(8,128)(2,1)S(1)}, u32[]{:S(2)}, u32[]{:S(2)}) collective-permute-start(bf16[128,720]{1,0:T(8,128)(2,1)S(1)} %get-tuple-element.27), channel_id=1, source_target_pairs={{0,1},{1,0},{2,3},{3,2},{4,5},{5,4},{6,7},{7,6},{8,9},{9,8},{10,11... | collective-permute-start | bytes 552968 | tf_op jit(solution)/shard_map/ppermute | solution.py:305
  44.5 7.2 %collective-permute-start.18 = (bf16[128,720]{1,0:T(8,128)(2,1)S(1)}, bf16[128,720]{1,0:T(8,128)(2,1)S(1)}, u32[]{:S(2)}, u32[]{:S(2)}) collective-permute-start(bf16[128,720]{1,0:T(8,128)(2,1)S(1)} %add_convert_fusion.3), channel_id=1, source_target_pairs={{0,2},{1,3},{2,0},{3,1},{4,6},{5,7},{6,4},{7,5},{8,10},{9,11},{10,... | collective-permute-start | bytes 552968 | tf_op jit(solution)/shard_map/ppermute | solution.py:305
  45.5 1.4 %collective-permute-start.24 = (bf16[128,720]{1,0:T(8,128)(2,1)S(1)}, bf16[128,720]{1,0:T(8,128)(2,1)S(1)}, u32[]{:S(2)}, u32[]{:S(2)}) collective-permute-start(bf16[128,720]{1,0:T(8,128)(2,1)S(1)} %get-tuple-element.30), channel_id=1, source_target_pairs={{0,1},{1,0},{2,3},{3,2},{4,5},{5,4},{6,7},{7,6},{8,9},{9,8},{10,11... | collective-permute-start | bytes 552968 | tf_op jit(solution)/shard_map/ppermute | solution.py:305
  45.7 7.3 %collective-permute-start.20 = (bf16[128,720]{1,0:T(8,128)(2,1)S(1)}, bf16[128,720]{1,0:T(8,128)(2,1)S(1)}, u32[]{:S(2)}, u32[]{:S(2)}) collective-permute-start(bf16[128,720]{1,0:T(8,128)(2,1)S(1)} %add_convert_fusion.2), channel_id=1, source_target_pairs={{0,4},{1,5},{2,6},{3,7},{4,0},{5,1},{6,2},{7,3},{8,12},{9,13},{10,... | collective-permute-start | bytes 552968 | tf_op jit(solution)/shard_map/ppermute | solution.py:305
  47.0 8.0 %collective-permute-start.25 = (bf16[32,720]{1,0:T(8,128)(2,1)S(1)}, bf16[32,720]{1,0:T(8,128)(2,1)S(1)}, u32[]{:S(2)}, u32[]{:S(2)}) collective-permute-start(bf16[32,720]{1,0:T(8,128)(2,1)S(1)} %get-tuple-element.34), channel_id=1, source_target_pairs={{0,8},{1,9},{2,10},{3,11},{4,12},{5,13},{6,14},{7,15},{8,0},{9,1},... | collective-permute-start | bytes 138248 | tf_op jit(solution)/shard_map/ppermute | solution.py:305
  47.1 9.5 %collective-permute-start.27 = (bf16[32,720]{1,0:T(8,128)(2,1)S(1)}, bf16[32,720]{1,0:T(8,128)(2,1)S(1)}, u32[]{:S(2)}, u32[]{:S(2)}) collective-permute-start(bf16[32,720]{1,0:T(8,128)(2,1)S(1)} %get-tuple-element.35), channel_id=1, source_target_pairs={{0,24},{1,25},{2,26},{3,27},{4,28},{5,29},{6,30},{7,31},{8,16},{9,... | collective-permute-start | bytes 138248 | tf_op jit(solution)/shard_map/ppermute | solution.py:305
  48.9 7.7 %collective-permute-start.26 = (bf16[32,720]{1,0:T(8,128)(2,1)S(1)}, bf16[32,720]{1,0:T(8,128)(2,1)S(1)}, u32[]{:S(2)}, u32[]{:S(2)}) collective-permute-start(bf16[32,720]{1,0:T(8,128)(2,1)S(1)} %get-tuple-element.36), channel_id=1, source_target_pairs={{0,16},{1,17},{2,18},{3,19},{4,20},{5,21},{6,22},{7,23},{8,24},{9,... | collective-permute-start | bytes 138248 | tf_op jit(solution)/shard_map/ppermute | solution.py:305
  53.1 5.2 %collective-permute-start.21 = (bf16[32,720]{1,0:T(8,128)(2,1)S(1)}, bf16[32,720]{1,0:T(8,128)(2,1)S(1)}, u32[]{:S(2)}, u32[]{:S(2)}) collective-permute-start(bf16[32,720]{1,0:T(8,128)(2,1)S(1)} %get-tuple-element.31), channel_id=1, source_target_pairs={{0,8},{1,9},{2,10},{3,11},{4,12},{5,13},{6,14},{7,15},{8,0},{9,1},... | collective-permute-start | bytes 138248 | tf_op jit(solution)/shard_map/ppermute | solution.py:305
  53.2 5.9 %collective-permute-start.23 = (bf16[32,720]{1,0:T(8,128)(2,1)S(1)}, bf16[32,720]{1,0:T(8,128)(2,1)S(1)}, u32[]{:S(2)}, u32[]{:S(2)}) collective-permute-start(bf16[32,720]{1,0:T(8,128)(2,1)S(1)} %get-tuple-element.32), channel_id=1, source_target_pairs={{0,24},{1,25},{2,26},{3,27},{4,28},{5,29},{6,30},{7,31},{8,16},{9,... | collective-permute-start | bytes 138248 | tf_op jit(solution)/shard_map/ppermute | solution.py:305
  55.0 5.9 %collective-permute-start.22 = (bf16[32,720]{1,0:T(8,128)(2,1)S(1)}, bf16[32,720]{1,0:T(8,128)(2,1)S(1)}, u32[]{:S(2)}, u32[]{:S(2)}) collective-permute-start(bf16[32,720]{1,0:T(8,128)(2,1)S(1)} %get-tuple-element.33), channel_id=1, source_target_pairs={{0,16},{1,17},{2,18},{3,19},{4,20},{5,21},{6,22},{7,23},{8,24},{9,... | collective-permute-start | bytes 138248 | tf_op jit(solution)/shard_map/ppermute | solution.py:305
  56.7 5.1 %collective-permute-start.28 = (bf16[32,720]{1,0:T(8,128)(2,1)S(1)}, bf16[32,720]{1,0:T(8,128)(2,1)S(1)}, u32[]{:S(2)}, u32[]{:S(2)}) collective-permute-start(bf16[32,720]{1,0:T(8,128)(2,1)S(1)} %add_convert_fusion.6), channel_id=1, source_target_pairs={{0,6},{1,7},{2,4},{3,5},{4,2},{5,3},{6,0},{7,1},{8,14},{9,15},{10,... | collective-permute-start | bytes 138248 | tf_op jit(solution)/shard_map/ppermute | solution.py:305
